TPU v7x, 256 devices: a whole 4x4x8 slice. The times are simulated.
256 devices in a mesh: cells: 64 (over z, y, core), grp: 4 (over x).
Axes of the slice: x: 4, y: 4, z: 8, core: 2. Of those that a mesh axis runs over, the one named last changes fastest.
Arguments:
- latent_coordinates: float32 [50, 1048576], P(None, ('cells', 'grp')), may hold values from -40 to 40
- group_means: float32 [128, 50], replicated, may hold values from -4 to 4
- entropy_scaling: float32 [128], replicated, may hold values from 0.5 to 2
- sample_shrinkage_lambda: float32 [200], replicated, may hold values from 1311 to 10485
- sample_population: int32 [200], replicated, may hold values from 1 to 10485, 1048576 in all
Outputs:
- corrected: float32 [50, 1048576], P(None, ('cells', 'grp'))
- new_centroids: float32 [128, 50], P('cells')
All inputs are finite; a program needn't handle non-finite values.
Results may differ from a plain program's by a relative error of at most 0.0003.
Values sent between devices are 32-bit elements; how exact they have to be, the bound alone decides.
A program may use at most 64 MiB of HBM per device.

v0:
```python
import functools

import jax
import jax.numpy as jnp
from jax import lax
from jax.experimental import pallas as pl
from jax.experimental.pallas import tpu as pltpu
from jax.sharding import Mesh
from jax.sharding import PartitionSpec as P

CELLS = ("cells_0", "cells_1", "cells_2")
CELLS_GRP = ("cells_0", "cells_1", "cells_2", "grp")


diversity = 2.0
intercept_ridge = 1.0
highest = lax.Precision.HIGHEST


def split_up(array, dim, size):
    dims = array.shape
    parts = array.reshape(*dims[:dim], size, dims[dim] // size, *dims[dim + 1 :])
    return jnp.moveaxis(parts, dim, 0)


def summed_on_arrival(array, axis, dim):
    size = lax.axis_size(axis)
    parts = lax.all_to_all(split_up(array, dim, size), axis, 0, 0, tiled=True)
    return jnp.sum(parts, axis=0)


def sum_in_two_steps(array, axes, dim):
    far, near = axes
    parts = split_up(array, dim, lax.axis_size(far))
    nearer = summed_on_arrival(parts, near, dim + 1)
    arrived = lax.all_to_all(nearer, far, split_axis=0, concat_axis=0, tiled=True)
    return arrived.sum(axis=0)


def filled_up(lines, size):
    spare = -len(lines) % size
    return jnp.pad(lines, [(0, spare)] + [(0, 0)] * (lines.ndim - 1))


def sent_to_all(array, axis):
    size = lax.axis_size(axis)
    return lax.all_to_all(
        jnp.broadcast_to(array[None], (size, *array.shape)), axis, 0, 0, tiled=True
    )


def joined_along(parts, dim):
    parts = jnp.moveaxis(parts, 0, dim)
    dims = parts.shape
    return parts.reshape(*dims[:dim], dims[dim] * dims[dim + 1], *dims[dim + 2 :])


def gather_axes(array, axes, dim):
    far, near = axes
    leading = sent_to_all(array, far)
    parts = jnp.swapaxes(sent_to_all(leading, near), 0, 1)
    return joined_along(parts.reshape(-1, *array.shape), dim)


def total_of(array, axes):
    lines = array.reshape(-1)
    own = sum_in_two_steps(
        filled_up(lines, lax.axis_size(axes[0]) * lax.axis_size(axes[1])), axes, 0
    )
    whole = gather_axes(own, axes, 0)
    return whole[: len(lines)].reshape(array.shape)


def from_behind(block, axis, distance):
    devices = range(lax.axis_size(axis))
    route = [(i - distance, i) for i in devices if i - distance in devices]
    return lax.ppermute(block, axis, route)


def by_axis(array, axes):
    return functools.reduce(lax.psum, axes, array)


def observation_affinity(latent_coordinates, group_means, entropy_scaling):
    pairwise_dots = jnp.dot(
        group_means, latent_coordinates, precision=highest, preferred_element_type=jnp.float32
    )
    quadratic_lengths = jnp.sum(group_means * group_means, axis=1)
    return (2.0 * pairwise_dots - quadratic_lengths[:, None]) / (2.0 * entropy_scaling[:, None])


def probabilistic_responsibility(group_affinity):
    top = jnp.max(group_affinity, axis=0, keepdims=True)
    raised = jnp.exp(group_affinity - top)
    return raised / jnp.sum(raised, axis=0, keepdims=True)


def batch_parts(moments, ridge):
    mass = moments[:, 0, :]
    sums = moments[:, 1:, :]
    shrink = ridge[None, :] / (mass + ridge[None, :])
    weight = jnp.sum(mass * shrink, axis=1)
    right_side = jnp.sum(sums * shrink[:, None, :], axis=2)
    return (weight, right_side, jnp.sum(mass, axis=1), jnp.sum(sums, axis=2))


def slopes_of(moments, ridge, weight, right_side):
    mass = moments[:, 0, :]
    sums = moments[:, 1:, :]
    intercept = right_side / (intercept_ridge + weight)[:, None]
    return (sums - mass[:, None, :] * intercept[:, :, None]) / (mass + ridge[None, :])[:, None, :]


def wide_body(
    latent_coordinates, group_means, entropy_scaling, sample_shrinkage_lambda, sample_population
):
    local_cells = latent_coordinates.shape[1]
    num_pcs = latent_coordinates.shape[0]
    clusters = group_means.shape[0]
    batches = sample_population.shape[0]
    owned = clusters // lax.axis_size(CELLS)
    offset = (lax.axis_index(CELLS) * lax.axis_size("grp") + lax.axis_index("grp")) * local_cells
    batch_ends = jnp.cumsum(sample_population)
    batch_starts = batch_ends - sample_population
    cells_total = jnp.sum(sample_population).astype(jnp.float32)
    position = offset + lax.iota(jnp.int32, local_cells)
    batch_of = jnp.sum((batch_ends[:, None] <= position[None, :]).astype(jnp.int32), axis=0)
    first_batch = batch_of[0]
    last_batch = batch_of[local_cells - 1]
    group_affinity = observation_affinity(latent_coordinates, group_means, entropy_scaling)
    expected_occupancy = probabilistic_responsibility(group_affinity)

    def count_step(batch_id, running):
        in_batch = (batch_of == batch_id).astype(jnp.float32)
        single_observation = jnp.dot(
            expected_occupancy, in_batch, precision=highest, preferred_element_type=jnp.float32
        )
        return lax.dynamic_update_slice(
            running, single_observation[:, None], (jnp.int32(0), batch_id)
        )

    counts = lax.fori_loop(
        first_batch, last_batch + 1, count_step, jnp.zeros((clusters, batches), jnp.float32)
    )
    counts = total_of(counts, (("cells_0", "cells_1"), ("cells_2", "grp")))
    totals = jnp.sum(counts, axis=1)
    expected = sample_population.astype(jnp.float32)[None, :] * totals[:, None] / cells_total
    penalty = diversity * jnp.log((counts + 1.0) / (expected + 1.0))

    def penalty_step(batch_id, running):
        in_batch = (batch_of == batch_id).astype(jnp.float32)
        column = lax.dynamic_index_in_dim(penalty, batch_id, 1, keepdims=True)
        return running + column * in_batch[None, :]

    cell_penalty = lax.fori_loop(
        first_batch, last_batch + 1, penalty_step, jnp.zeros((clusters, local_cells), jnp.float32)
    )
    assign = probabilistic_responsibility(group_affinity - cell_penalty)
    augmented = jnp.concatenate(
        [jnp.ones((1, local_cells), jnp.float32), latent_coordinates], axis=0
    )

    def moment_step(batch_id, running):
        in_batch = (batch_of == batch_id).astype(jnp.float32)
        contiguous_portion = jnp.einsum(
            "kn,dn->kd", assign * in_batch[None, :], augmented, precision=highest
        )
        return lax.dynamic_update_slice(
            running, contiguous_portion[:, :, None], (jnp.int32(0), jnp.int32(0), batch_id)
        )

    moments = lax.fori_loop(
        first_batch,
        last_batch + 1,
        moment_step,
        jnp.zeros((clusters, num_pcs + 1, batches), jnp.float32),
    )
    devices_flat = lax.axis_size(CELLS) * lax.axis_size("grp")
    most_cells = 2 * local_cells * devices_flat // batches
    reach = (most_cells - 2) // local_cells + 1
    begins_here = (batch_starts >= offset) & (batch_starts < offset + local_cells)
    owner_mask = begins_here.astype(jnp.float32)
    head_owned = begins_here[first_batch]
    head_column = lax.dynamic_index_in_dim(moments, first_batch, 2, keepdims=False)
    sent_stats = jnp.where(head_owned, 0.0, 1.0) * head_column
    sent_tag = jnp.where(head_owned, 0.0, first_batch.astype(jnp.float32) + 1.0) * jnp.ones(
        (1,), jnp.float32
    )
    completed = moments
    for hop in range(1, reach + 1):
        got_stats, got_tag = from_behind((sent_stats, sent_tag), CELLS_GRP, -hop)
        got_id = jnp.maximum(got_tag[0].astype(jnp.int32) - 1, 0)
        accept = jnp.where((got_tag[0] > 0.5) & begins_here[got_id], 1.0, 0.0)
        single_observation = (
            lax.dynamic_index_in_dim(completed, got_id, 2, keepdims=False) + accept * got_stats
        )
        completed = lax.dynamic_update_slice(
            completed, single_observation[:, :, None], (jnp.int32(0), jnp.int32(0), got_id)
        )
    completed = completed * owner_mask[None, None, :]
    weight, right_side, mass_total, moment_total = jax.tree.map(
        lambda part: by_axis(part, CELLS_GRP), batch_parts(completed, sample_shrinkage_lambda)
    )
    coefficients = slopes_of(completed, sample_shrinkage_lambda, weight, right_side)
    every_centroid = moment_total / (1.0 + mass_total)[:, None]
    new_centroids = lax.dynamic_slice_in_dim(
        every_centroid, lax.axis_index(CELLS) * owned, owned, 0
    )
    tail_owned = begins_here[last_batch]
    tail_column = lax.dynamic_index_in_dim(coefficients, last_batch, 2, keepdims=False)
    tail_send = jnp.where(tail_owned, 1.0, 0.0) * tail_column
    tail_tag = jnp.where(tail_owned, last_batch.astype(jnp.float32) + 1.0, 0.0) * jnp.ones(
        (1,), jnp.float32
    )
    head_fix = jnp.zeros_like(tail_column)
    for hop in range(1, reach + 1):
        got_coef, got_tag = from_behind((tail_send, tail_tag), CELLS_GRP, hop)
        match = got_tag[0] == first_batch.astype(jnp.float32) + 1.0
        head_fix = jnp.where(match, got_coef, head_fix)
    own_head = lax.dynamic_index_in_dim(coefficients, first_batch, 2, keepdims=False)
    head_final = jnp.where(head_owned, own_head, head_fix)
    coefficients = lax.dynamic_update_slice(
        coefficients, head_final[:, :, None], (jnp.int32(0), jnp.int32(0), first_batch)
    )

    def correct_step(batch_id, running):
        in_batch = (batch_of == batch_id).astype(jnp.float32)
        slope_table = lax.dynamic_index_in_dim(coefficients, batch_id, 2, keepdims=False)
        moved = jnp.einsum("kd,kn->dn", slope_table, assign * in_batch[None, :], precision=highest)
        return running - moved

    corrected = lax.fori_loop(first_batch, last_batch + 1, correct_step, latent_coordinates)
    return (latent_coordinates - corrected, new_centroids)


SLOTS = 8
ROWS = 64
MOST = 10485
MESH = pl.DeviceIdType.MESH
bf16, f32 = jnp.bfloat16, jnp.float32


def two_pieces(value):
    first = value.astype(bf16)
    return first, (value - first.astype(f32)).astype(bf16)


def across(left, right):
    return lax.dot_general(left, right, (((1,), (1,)), ((), ())), preferred_element_type=f32)


def plain(left, right):
    return jnp.dot(left, right, preferred_element_type=f32)


def step_kernel(
    shape,
    cells_all,
    z_hbm,
    means_ref,
    soft_ref,
    ridge_ref,
    pop_ref,
    moved_ref,
    cent_ref,
    zf,
    zc,
    ex,
    pair,
    means_wide,
    acc,
    slopes,
    near_out,
    near_counts,
    near_mass,
    near_moments,
    ends_out,
    line_a,
    line_b,
    sums_out,
    sum_in,
    cent_out,
    cent_in,
    tile_out,
    tile_in,
    full_sums,
    load_sems,
    send_sems,
    recv_sems,
):
    nz, ny, nc, nx = shape
    near = nc * nx
    far = nz * ny
    count = near * far
    cells = zf.shape[1]
    pcs = means_ref.shape[1]
    clusters = means_ref.shape[0]
    batches = pop_ref.shape[1]
    rows_each = ROWS // near
    reach = (MOST - 2) // cells + 1
    offsets = [h for h in range(-reach, reach + 1) if h]
    me = (
        (lax.axis_index("cells_0") * ny + lax.axis_index("cells_1")) * nc
        + lax.axis_index("cells_2")
    ) * nx + lax.axis_index("grp")
    rank = lax.rem(me, near)
    block = lax.div(me, near)

    def place(q):
        return (
            lax.div(q, ny * nc * nx),
            lax.rem(lax.div(q, nc * nx), ny),
            lax.rem(lax.div(q, nx), nc),
            lax.rem(q, nx),
        )

    def mate(r):
        return block * near + lax.rem(rank + r, near)

    def peer(r):
        return lax.rem(block + r, far) * near + rank

    def neighbour(h):
        return lax.rem(me + (h + count), count)

    def push(src, dst, which, q):
        pltpu.make_async_remote_copy(
            src_ref=src,
            dst_ref=dst,
            send_sem=send_sems.at[which],
            recv_sem=recv_sems.at[which],
            device_id=place(q),
            device_id_type=MESH,
        ).start()

    def arrived(buffer, which):
        pltpu.make_async_copy(buffer, buffer, recv_sems.at[which]).wait()

    def left(buffer, which):
        pltpu.make_async_copy(buffer, buffer, send_sems.at[which]).wait()

    barrier = pltpu.get_barrier_semaphore()
    for r in range(1, near):
        pl.semaphore_signal(barrier, inc=1, device_id=place(mate(r)), device_id_type=MESH)
    for h in offsets:
        pl.semaphore_signal(barrier, inc=1, device_id=place(neighbour(h)), device_id_type=MESH)

    def greet(r, carry):
        pl.semaphore_signal(barrier, inc=1, device_id=place(peer(r)), device_id_type=MESH)
        return carry

    lax.fori_loop(1, far, greet, 0)

    loads = load_sems.shape[0]
    part = cells // loads
    for i in range(loads):
        columns = pl.ds(i * part, part)
        pltpu.make_async_copy(z_hbm.at[:, columns], zf.at[:, columns], load_sems.at[i]).start()

    means_wide[...] = jnp.zeros_like(means_wide)
    means_wide[:, 0:pcs] = means_ref[...]
    g = means_wide[...]
    square = lax.broadcasted_iota(jnp.int32, (clusters, clusters), 0)
    lane = lax.broadcasted_iota(jnp.int32, (clusters, clusters), 1)
    soft = jnp.sum(jnp.where(square == lane, soft_ref[...], 0.0), axis=1, keepdims=True)
    offset_of = -0.5 * jnp.sum(g * g, axis=1, keepdims=True) / soft
    weights = jnp.where(lane == pcs, offset_of, g / soft)
    w1 = weights.astype(bf16).astype(f32)
    w2 = (weights - w1).astype(bf16).astype(f32)
    o1 = offset_of.astype(bf16).astype(f32)
    o2 = (offset_of - o1).astype(bf16).astype(f32)
    w1 = jnp.where(lane == pcs + 1, offset_of - o1 - o2, w1)
    w1 = (w1 + pltpu.roll(w1, ROWS, 1)).astype(bf16)
    w2 = (w2 + pltpu.roll(w2, ROWS, 1)).astype(bf16)
    weights = jnp.concatenate([w1, w2], axis=1)

    pop = pop_ref[...].astype(f32)
    up = lax.broadcasted_iota(jnp.int32, (batches, batches), 0)
    down = lax.broadcasted_iota(jnp.int32, (batches, batches), 1)
    ends = jnp.dot(
        jnp.broadcast_to(pop, (8, batches)),
        (up <= down).astype(f32),
        precision=highest,
        preferred_element_type=f32,
    )[0:1]
    half = lax.broadcasted_iota(jnp.int32, (16, 1), 0)
    device = me + lax.rem(half, 8) - reach
    limit = device * cells + jnp.where(half >= 8, cells - 1, 0)
    spot = jnp.sum((ends <= limit.astype(f32)).astype(f32), axis=1, keepdims=True)
    spot = jnp.where(device < 0, -9.0, spot)
    first = {h: spot[h + reach : h + reach + 1] for h in offsets + [0]}
    last = {h: spot[8 + h + reach : 9 + h + reach] for h in offsets + [0]}
    slot = lax.broadcasted_iota(jnp.int32, (SLOTS, 1), 0).astype(f32)
    batch_id = first[0] + slot
    chosen = lax.broadcasted_iota(jnp.int32, (SLOTS, batches), 1).astype(f32) == batch_id
    held = jnp.sum(jnp.where(chosen, pop, 0.0), axis=1, keepdims=True)
    ridge = jnp.sum(jnp.where(chosen, ridge_ref[...], 0.0), axis=1, keepdims=True)
    ridge = jnp.where(batch_id < batches, ridge, 1.0)
    stop = jnp.sum(jnp.where(chosen, ends, 0.0), axis=1, keepdims=True) - (me * cells).astype(f32)
    start = stop - held
    tail = slot == last[0] - first[0]
    head = slot == 0.0
    behind = {h: (last[h] == first[0]).astype(f32) for h in offsets if h < 0}
    ahead = {h: (first[h] == last[0]).astype(f32) for h in offsets if h > 0}

    def inside(c, width, times):
        position = (
            lax.broadcasted_iota(jnp.int32, (SLOTS * times, width), 1) + c * width
        ).astype(f32)
        low = jnp.concatenate([start] * times, axis=0)
        high = jnp.concatenate([stop] * times, axis=0)
        return ((position >= low) & (position < high)).astype(f32)

    def completed(own, buffer, tail_row):
        before = jnp.zeros((1, clusters), f32)
        after = jnp.zeros((1, clusters), f32)
        for i, h in enumerate(offsets):
            if h < 0:
                before = before + behind[h] * buffer[i, 1:2, :]
            else:
                after = after + ahead[h] * buffer[i, 0:1, :]
        return own + jnp.where(head, before, 0.0) + jnp.where(tail, after, 0.0)

    def rows_of(*lines):
        row = lax.broadcasted_iota(jnp.int32, (8, clusters), 0)
        value = jnp.zeros((8, clusters), f32)
        for i, line in enumerate(lines):
            value = jnp.where(row == i, line, value)
        return value

    width = 512
    per_load = part // width

    for i in range(loads):
        columns = pl.ds(i * part, part)
        pltpu.make_async_copy(z_hbm.at[:, columns], zf.at[:, columns], load_sems.at[i]).wait()

    def prior_step(c, total):
        columns = pl.ds(pl.multiple_of(c * width, width), width)
        z1, z2 = two_pieces(
            jnp.concatenate(
                [
                    zf[:, columns],
                    jnp.ones((2, width), f32),
                    jnp.zeros((ROWS - 2 - pcs, width), f32),
                ],
                axis=0,
            )
        )
        zc[0:ROWS, columns] = z1
        zc[ROWS : 2 * ROWS, columns] = z2
        score = plain(weights, jnp.concatenate([z1, z2, z1, z2], axis=0))
        raised = jnp.exp(score - jnp.max(score, axis=0, keepdims=True))
        ex[:, columns] = raised
        p1, p2 = two_pieces(raised * (1.0 / jnp.sum(raised, axis=0, keepdims=True)))
        mask = inside(c, width, 2).astype(bf16)
        return total + across(mask, jnp.concatenate([p1, p2], axis=0))

    total = lax.fori_loop(
        0, cells // width, prior_step, jnp.zeros((2 * SLOTS, 2 * clusters), f32)
    )
    counts = total[0:SLOTS, 0:clusters] + total[0:SLOTS, clusters : 2 * clusters]
    own_total = jnp.sum(counts, axis=0, keepdims=True)
    near_out[0] = rows_of(
        counts[0:1], jnp.sum(jnp.where(tail, counts, 0.0), axis=0, keepdims=True), own_total
    )
    pl.semaphore_wait(barrier, near - 1 + far - 1 + len(offsets))
    for r in range(1, near):
        push(near_out.at[0], line_a.at[r - 1], 0, mate(r))
    for i, h in enumerate(offsets):
        push(near_out.at[0], near_counts.at[len(offsets) - 1 - i], 1, neighbour(h))
    arrived(line_a, 0)
    block_total = own_total
    for r in range(near - 1):
        block_total = block_total + line_a[r, 2:3, :]
    tile_out[0] = jnp.broadcast_to(block_total, (8, clusters))

    def send_line(r, carry):
        push(tile_out.at[0], line_b.at[r - 1], 2, peer(r))
        return carry

    lax.fori_loop(1, far, send_line, 0)
    arrived(near_counts, 1)
    full_counts = completed(counts, near_counts, 1)
    arrived(line_b, 2)
    totals = block_total + jnp.sum(line_b[...], axis=0)[0:1]
    expected = held * totals * (1.0 / cells_all)
    ratio = (expected + 1.0) / (full_counts + 1.0)
    factor = ratio * ratio
    f1 = factor.astype(bf16).astype(f32)
    f2 = (factor - f1).astype(bf16).astype(f32)
    f3 = factor - f1 - f2
    factor = jnp.concatenate([f1, f2, f3, jnp.zeros_like(f3)], axis=0).T.astype(bf16)

    acc[...] = jnp.zeros_like(acc)

    def moment_step(c, carry):
        columns = pl.ds(pl.multiple_of(c * width, width), width)
        mask = inside(c, width, 4).astype(bf16)
        weighed = ex[:, columns] * plain(factor, mask)
        a1, a2 = two_pieces(weighed * (1.0 / jnp.sum(weighed, axis=0, keepdims=True)))
        pair[0:clusters, columns] = a1
        pair[clusters : 2 * clusters, columns] = a2
        z = zc[:, columns]
        both = jnp.concatenate([a1, a2], axis=0)
        lined = jnp.concatenate([z * mask[s : s + 1, :] for s in range(SLOTS)], axis=0)
        acc[...] += across(lined, both)
        return carry

    lax.fori_loop(0, cells // width, moment_step, 0)
    moments = []
    for s in range(SLOTS):
        top = acc[2 * ROWS * s : 2 * ROWS * s + ROWS, :]
        low = acc[2 * ROWS * s + ROWS : 2 * ROWS * (s + 1), :]
        moments.append(
            top[:, 0:clusters] + top[:, clusters:] + low[:, 0:clusters] + low[:, clusters:]
        )
    mass = rows_of(*[moments[s][pcs : pcs + 1] for s in range(SLOTS)])
    near_out[1] = rows_of(
        mass[0:1], jnp.sum(jnp.where(tail, mass, 0.0), axis=0, keepdims=True)
    )
    for i, h in enumerate(offsets):
        push(near_out.at[1], near_mass.at[len(offsets) - 1 - i], 3, neighbour(h))
    whole = moments[0]
    tail_moment = moments[0] * tail[0:1].astype(f32)
    for s in range(1, SLOTS):
        whole = whole + moments[s]
        tail_moment = tail_moment + moments[s] * tail[s : s + 1].astype(f32)
    ends_out[0] = moments[0][0:56]
    ends_out[1] = tail_moment[0:56]
    for t in range(near):
        cent_out[t] = whole[t * rows_each : (t + 1) * rows_each]
    for r in range(1, near):
        push(cent_out.at[lax.rem(rank + r, near)], cent_in.at[r - 1], 4, mate(r))
    arrived(near_mass, 3)
    full_mass = completed(mass, near_mass, 1)
    shrink = ridge / (full_mass + ridge)
    right = moments[0] * shrink[0:1]
    for s in range(1, SLOTS):
        right = right + moments[s] * shrink[s : s + 1]
    for t in range(near):
        sums_out[t] = right[t * rows_each : (t + 1) * rows_each]
    for r in range(1, near):
        push(sums_out.at[lax.rem(rank + r, near)], sum_in.at[r - 1], 5, mate(r))
    for i, h in enumerate(offsets):
        push(ends_out.at[int(h > 0)], near_moments.at[len(offsets) - 1 - i], 6, neighbour(h))
    arrived(cent_in, 4)
    cent_tile = cent_out[rank]
    for r in range(near - 1):
        cent_tile = cent_tile + cent_in[r]
    tile_out[1] = cent_tile
    arrived(sum_in, 5)
    sum_tile = sums_out[rank]
    for r in range(near - 1):
        sum_tile = sum_tile + sum_in[r]
    tile_out[2] = sum_tile

    def send_sum(r, carry):
        push(tile_out.at[2], tile_in.at[1, r - 1], 8, peer(r))
        return carry

    def send_cent(r, carry):
        push(tile_out.at[1], tile_in.at[0, r - 1], 7, peer(r))
        return carry

    lax.fori_loop(1, far, send_sum, 0)
    lax.fori_loop(1, far, send_cent, 0)

    arrived(near_moments, 6)
    before = jnp.zeros((56, clusters), f32)
    after = jnp.zeros((56, clusters), f32)
    for i, h in enumerate(offsets):
        if h < 0:
            before = before + behind[h] * near_moments[i]
        else:
            after = after + ahead[h] * near_moments[i]

    arrived(tile_in.at[1], 8)
    full_sums[1, 0] = sum_tile + jnp.sum(tile_in[1], axis=0)
    for r in range(1, near):
        push(full_sums.at[1, 0], full_sums.at[1, r], 10, mate(r))
    arrived(tile_in.at[0], 7)
    full_sums[0, 0] = cent_tile + jnp.sum(tile_in[0], axis=0)
    for r in range(1, near):
        push(full_sums.at[0, 0], full_sums.at[0, r], 9, mate(r))

    def gathered(which):
        return jnp.concatenate(
            [full_sums[which, lax.rem(rank + (near - t), near)] for t in range(near)], axis=0
        )

    arrived(full_sums.at[1, pl.ds(1, near - 1)], 10)
    right = gathered(1)
    intercept = (right / (1.0 + right[pcs : pcs + 1]))[0:56]
    for s in range(SLOTS):
        moment = moments[s][0:56] + after * tail[s : s + 1].astype(f32)
        if s == 0:
            moment = moment + before
        line = full_mass[s : s + 1]
        slope = (moment - line * intercept) / (line + ridge[s : s + 1])
        c1, c2 = two_pieces(jnp.concatenate([slope, jnp.zeros((8, clusters), f32)], axis=0))
        slopes[ROWS * s : ROWS * (s + 1), :] = jnp.concatenate([c1, c1, c2], axis=1)

    def moved_step(c, carry):
        columns = pl.ds(pl.multiple_of(c * width, width), width)
        both = pair[:, columns]
        every = plain(slopes[...], jnp.concatenate([both, both[0:clusters]], axis=0))
        mask = inside(c, width, 1)
        moved = every[0:ROWS] * mask[0:1]
        for s in range(1, SLOTS):
            moved = moved + every[ROWS * s : ROWS * (s + 1)] * mask[s : s + 1]
        moved_ref[:, columns] = moved[0:pcs]
        return carry

    lax.fori_loop(0, cells // width, moved_step, 0)

    arrived(full_sums.at[0, pl.ds(1, near - 1)], 9)
    centre = gathered(0)
    centre = (centre / (1.0 + centre[pcs : pcs + 1])).T
    owned = cent_ref.shape[0]
    cells_at = lax.div(me, nx)
    row = lax.broadcasted_iota(jnp.int32, (clusters, ROWS), 0)
    for j in range(owned):
        line = jnp.sum(jnp.where(row == cells_at * owned + j, centre, 0.0), axis=0, keepdims=True)
        cent_ref[j : j + 1, :] = line[:, 0:pcs]

    left(line_a, 0)
    left(near_counts, 1)
    left(line_b, 2)
    left(near_mass, 3)
    left(cent_in, 4)
    left(sum_in, 5)
    left(near_moments, 6)
    left(tile_in.at[0], 7)
    left(tile_in.at[1], 8)
    left(full_sums.at[0, pl.ds(1, near - 1)], 9)
    left(full_sums.at[1, pl.ds(1, near - 1)], 10)


def narrow_body(
    shape, latent_coordinates, group_means, entropy_scaling, sample_shrinkage_lambda, sample_population
):
    pcs, cells = latent_coordinates.shape
    clusters = group_means.shape[0]
    batches = sample_population.shape[0]
    nz, ny, nc, nx = shape
    near, far = nc * nx, nz * ny
    rows_each = ROWS // near
    reach = (MOST - 2) // cells + 1
    owned = clusters // (nz * ny * nc)
    vmem = pl.BlockSpec(memory_space=pltpu.VMEM)
    scratch = [
        pltpu.VMEM((pcs, cells), f32),
        pltpu.VMEM((2 * ROWS, cells), bf16),
        pltpu.VMEM((clusters, cells), f32),
        pltpu.VMEM((2 * clusters, cells), bf16),
        pltpu.VMEM((clusters, clusters), f32),
        pltpu.VMEM((SLOTS * 2 * ROWS, 2 * clusters), f32),
        pltpu.VMEM((SLOTS * ROWS, 3 * clusters), bf16),
        pltpu.VMEM((2, 8, clusters), f32),
        pltpu.VMEM((2 * reach, 8, clusters), f32),
        pltpu.VMEM((2 * reach, 8, clusters), f32),
        pltpu.VMEM((2 * reach, 56, clusters), f32),
        pltpu.VMEM((2, 56, clusters), f32),
        pltpu.VMEM((near - 1, 8, clusters), f32),
        pltpu.VMEM((far - 1, 8, clusters), f32),
        pltpu.VMEM((near, rows_each, clusters), f32),
        pltpu.VMEM((near - 1, rows_each, clusters), f32),
        pltpu.VMEM((near, rows_each, clusters), f32),
        pltpu.VMEM((near - 1, rows_each, clusters), f32),
        pltpu.VMEM((3, rows_each, clusters), f32),
        pltpu.VMEM((2, far - 1, rows_each, clusters), f32),
        pltpu.VMEM((2, near, rows_each, clusters), f32),
        pltpu.SemaphoreType.DMA((4,)),
        pltpu.SemaphoreType.DMA((11,)),
        pltpu.SemaphoreType.DMA((11,)),
    ]
    return pl.pallas_call(
        functools.partial(step_kernel, shape, float(cells * near * far)),
        out_shape=(
            jax.ShapeDtypeStruct((pcs, cells), f32),
            jax.ShapeDtypeStruct((owned, pcs), f32),
        ),
        in_specs=[pl.BlockSpec(memory_space=pl.ANY)] + [vmem] * 4,
        out_specs=(vmem, vmem),
        scratch_shapes=scratch,
        compiler_params=pltpu.CompilerParams(
            collective_id=0, has_side_effects=True, vmem_limit_bytes=40 * 1024 * 1024
        ),
    )(
        latent_coordinates,
        group_means,
        entropy_scaling.reshape(1, clusters),
        sample_shrinkage_lambda.reshape(1, batches),
        sample_population.reshape(1, batches),
    )


def body(
    shape, latent_coordinates, group_means, entropy_scaling, sample_shrinkage_lambda, sample_population
):
    cells = latent_coordinates.shape[1]
    batches = sample_population.shape[0]
    inner = SLOTS - 1
    window = sample_population[: batches - inner + 1]
    for i in range(1, inner):
        window = window + sample_population[i : batches - inner + 1 + i]
    few = jnp.min(window) >= cells - 1
    moved, new_centroids = lax.cond(
        few,
        functools.partial(narrow_body, shape),
        wide_body,
        latent_coordinates,
        group_means,
        entropy_scaling,
        sample_shrinkage_lambda,
        sample_population,
    )
    return (latent_coordinates - moved, new_centroids)


def solution(mesh):
    shape = (mesh.shape["cells"] // 8, 4, 2, mesh.shape["grp"])
    finer = Mesh(mesh.devices.reshape(shape), ("cells_0", "cells_1", "cells_2", "grp"))
    return jax.shard_map(
        functools.partial(body, shape),
        mesh=finer,
        in_specs=(P(None, CELLS_GRP), P(), P(), P(), P()),
        out_specs=(P(None, CELLS_GRP), P(CELLS, None)),
        check_vma=False,
    )
```

profile of v0, /device:TPU:1, one launch (start us, length us, event | category | flops | bytes accessed | tf_op | source)
XLA Modules:
  0.0 59.0 jit_solution(8504705676659931830)
XLA Ops:
  0.6 1.6 %add_reduce_fusion = s32[]{:T(128)} fusion(s32[200]{0:T(256)} %param.19), kind=kLoop, calls=%fused_computation.63 | loop fusion | flops 1357 | bytes 5436 | tf_op jit(solution)/shard_map/reduce_min | solution.py:708
  2.9 53.3 %conditional.1 = ((f32[50,4096]{1,0:T(8,128)S(1)}, f32[2,50]{1,0:T(2,128)S(1)})) conditional(s32[]{:T(128)} %convert_element_type.58, (s32[200]{0:T(256)}, f32[128,50]{0,1:T(8,128)}, f32[50,4096]{1,0:T(8,128)}, f32[128]{0:T(128)}, f32[200]{0:T(256)}) %tuple.31, (f32[128]{0:T(128)}, f32[200]{0:T(256)}, s32[200]{0:T(256)}, f32[50,4096]{1,0:T(8,128)}, ...), branch_computations={%region_1.43_spmd, %region_43.44_spmd} | conditional | flops 978158016 | bytes 143480160 | solution.py:709
  3.2 0.8 %copy.61.means_ref = f32[128,50]{1,0:T(8,128)S(1)} copy(f32[128,50]{0,1:T(8,128)} %get-tuple-element.261) | data formatting | bytes 51200 | tf_op jit(solution)/shard_map
  4.0 52.2 %branch_1_fun.1 = (f32[50,4096]{1,0:T(8,128)S(1)}, f32[2,50]{1,0:T(2,128)S(1)}) custom-call(f32[50,4096]{1,0:T(8,128)} %get-tuple-element.147.z_hbm, f32[128,50]{1,0:T(8,128)S(1)} %copy.61.means_ref, f32[1,128]{1,0:T(1,128)} %bitcast.103, f32[1,200]{1,0:T(1,128)} %bitcast.101, s32[1,200]{1,0:T(1,128)} %bitcast.96), custom_call_target="tpu_custom_call" | custom-call | tf_op jit(solution)/shard_map/cond/branch_1_fun/pallas_call | solution.py:678
  56.3 2.2 %sub.51 = f32[50,4096]{1,0:T(8,128)} subtract(f32[50,4096]{1,0:T(8,128)} %param.15, f32[50,4096]{1,0:T(8,128)S(1)} %get-tuple-element.156) | non-fusion elementwise | flops 204800 | bytes 2457600 | tf_op jit(solution)/shard_map/sub | solution.py:719
  58.5 0.6 copy.115
where the time goes:
time: 59.3 us; the launch traced here: 59 us
  Pallas kernels  52.2 us (88%)
  other arithmetic  3.84 us (6%)
  local copies, waits for them, and re-layouts  1.41 us (2%)
  between operations  1.29 us (2%)
    pallas_call x1, Pallas kernels, narrow_body(): pl.pallas_call(functools.partial(step_kernel, shape, float(cells * near *...  52.2 us
    sub x1, other arithmetic, body(): return (latent_coordinates - moved, new_centroids)  2.2 us
    reduce_min x1, other arithmetic, body(): few = jnp.min(window) >= cells - 1  1.65 us

commit v1 on v0

--- a/solution.py
+++ b/solution.py
@@ -227,16 +227,18 @@
         in_batch = (batch_of == batch_id).astype(jnp.float32)
         slope_table = lax.dynamic_index_in_dim(coefficients, batch_id, 2, keepdims=False)
         moved = jnp.einsum("kd,kn->dn", slope_table, assign * in_batch[None, :], precision=highest)
-        return running - moved
-
-    corrected = lax.fori_loop(first_batch, last_batch + 1, correct_step, latent_coordinates)
+        return running + moved
+
+    corrected = lax.fori_loop(first_batch, last_batch + 1, correct_step, jnp.zeros_like(latent_coordinates))
     return (latent_coordinates - corrected, new_centroids)
 
 
 SLOTS = 8
 ROWS = 64
 MOST = 10485
-MESH = pl.DeviceIdType.MESH
+LOGICAL = pl.DeviceIdType.LOGICAL
+TILE = 256
+CLOSE = 4
 bf16, f32 = jnp.bfloat16, jnp.float32
 
 
@@ -261,15 +263,16 @@
     soft_ref,
     ridge_ref,
     pop_ref,
-    moved_ref,
+    zf,
+    pair,
+    slopes,
+    starts_ref,
+    flag_ref,
     cent_ref,
-    zf,
     zc,
     ex,
-    pair,
     means_wide,
-    acc,
-    slopes,
+    pieces,
     near_out,
     near_counts,
     near_mass,
@@ -293,10 +296,10 @@
     far = nz * ny
     count = near * far
     cells = zf.shape[1]
-    pcs = means_ref.shape[1]
-    clusters = means_ref.shape[0]
+    pcs, clusters = means_ref.shape
     batches = pop_ref.shape[1]
     rows_each = ROWS // near
+    width = 512
     reach = (MOST - 2) // cells + 1
     offsets = [h for h in range(-reach, reach + 1) if h]
     me = (
@@ -306,14 +309,6 @@
     rank = lax.rem(me, near)
     block = lax.div(me, near)
 
-    def place(q):
-        return (
-            lax.div(q, ny * nc * nx),
-            lax.rem(lax.div(q, nc * nx), ny),
-            lax.rem(lax.div(q, nx), nc),
-            lax.rem(q, nx),
-        )
-
     def mate(r):
         return block * near + lax.rem(rank + r, near)
 
@@ -329,8 +324,8 @@
             dst_ref=dst,
             send_sem=send_sems.at[which],
             recv_sem=recv_sems.at[which],
-            device_id=place(q),
-            device_id_type=MESH,
+            device_id=q,
+            device_id_type=LOGICAL,
         ).start()
 
     def arrived(buffer, which):
@@ -338,28 +333,28 @@
 
     def left(buffer, which):
         pltpu.make_async_copy(buffer, buffer, send_sems.at[which]).wait()
-
-    barrier = pltpu.get_barrier_semaphore()
-    for r in range(1, near):
-        pl.semaphore_signal(barrier, inc=1, device_id=place(mate(r)), device_id_type=MESH)
-    for h in offsets:
-        pl.semaphore_signal(barrier, inc=1, device_id=place(neighbour(h)), device_id_type=MESH)
-
-    def greet(r, carry):
-        pl.semaphore_signal(barrier, inc=1, device_id=place(peer(r)), device_id_type=MESH)
-        return carry
-
-    lax.fori_loop(1, far, greet, 0)
 
     loads = load_sems.shape[0]
     part = cells // loads
     for i in range(loads):
         columns = pl.ds(i * part, part)
-        pltpu.make_async_copy(z_hbm.at[:, columns], zf.at[:, columns], load_sems.at[i]).start()
+        pltpu.make_async_copy(z_hbm.at[0, :, columns], zf.at[:, columns], load_sems.at[i]).start()
+
+    barrier = pltpu.get_barrier_semaphore()
+    for r in range(1, near):
+        pl.semaphore_signal(barrier, inc=1, device_id=mate(r), device_id_type=LOGICAL)
+    for h in offsets:
+        pl.semaphore_signal(barrier, inc=1, device_id=neighbour(h), device_id_type=LOGICAL)
+
+    def greet(r, carry):
+        pl.semaphore_signal(barrier, inc=1, device_id=peer(r), device_id_type=LOGICAL)
+        return carry
+
+    lax.fori_loop(1, far, greet, 0)
 
     means_wide[...] = jnp.zeros_like(means_wide)
-    means_wide[:, 0:pcs] = means_ref[...]
-    g = means_wide[...]
+    means_wide[0:pcs, :] = means_ref[...]
+    g = means_wide[...].T
     square = lax.broadcasted_iota(jnp.int32, (clusters, clusters), 0)
     lane = lax.broadcasted_iota(jnp.int32, (clusters, clusters), 1)
     soft = jnp.sum(jnp.where(square == lane, soft_ref[...], 0.0), axis=1, keepdims=True)
@@ -374,39 +369,45 @@
     w2 = (w2 + pltpu.roll(w2, ROWS, 1)).astype(bf16)
     weights = jnp.concatenate([w1, w2], axis=1)
 
-    pop = pop_ref[...].astype(f32)
+    pop = pop_ref[...]
     up = lax.broadcasted_iota(jnp.int32, (batches, batches), 0)
     down = lax.broadcasted_iota(jnp.int32, (batches, batches), 1)
-    ends = jnp.dot(
-        jnp.broadcast_to(pop, (8, batches)),
-        (up <= down).astype(f32),
-        precision=highest,
-        preferred_element_type=f32,
-    )[0:1]
+    column = jnp.sum(jnp.where(up == down, pop, 0), axis=1, keepdims=True)
+    ends = jnp.sum(jnp.where(up <= down, column, 0), axis=0, keepdims=True)
     half = lax.broadcasted_iota(jnp.int32, (16, 1), 0)
     device = me + lax.rem(half, 8) - reach
     limit = device * cells + jnp.where(half >= 8, cells - 1, 0)
-    spot = jnp.sum((ends <= limit.astype(f32)).astype(f32), axis=1, keepdims=True)
-    spot = jnp.where(device < 0, -9.0, spot)
+    spot = jnp.sum(jnp.where(ends <= limit, 1, 0), axis=1, keepdims=True)
+    spot = jnp.where(device < 0, -9, spot)
     first = {h: spot[h + reach : h + reach + 1] for h in offsets + [0]}
     last = {h: spot[8 + h + reach : 9 + h + reach] for h in offsets + [0]}
-    slot = lax.broadcasted_iota(jnp.int32, (SLOTS, 1), 0).astype(f32)
+    slot = lax.broadcasted_iota(jnp.int32, (SLOTS, 1), 0)
     batch_id = first[0] + slot
-    chosen = lax.broadcasted_iota(jnp.int32, (SLOTS, batches), 1).astype(f32) == batch_id
-    held = jnp.sum(jnp.where(chosen, pop, 0.0), axis=1, keepdims=True)
+    batch_lane = lax.broadcasted_iota(jnp.int32, (SLOTS, batches), 1)
+    chosen = batch_lane == batch_id
+    held = jnp.sum(jnp.where(chosen, pop, 0), axis=1, keepdims=True)
     ridge = jnp.sum(jnp.where(chosen, ridge_ref[...], 0.0), axis=1, keepdims=True)
     ridge = jnp.where(batch_id < batches, ridge, 1.0)
-    stop = jnp.sum(jnp.where(chosen, ends, 0.0), axis=1, keepdims=True) - (me * cells).astype(f32)
+    stop = jnp.sum(jnp.where(batch_lane <= batch_id, pop, 0), axis=1, keepdims=True) - me * cells
     start = stop - held
+    held = held.astype(f32)
+    starts_ref[...] = jnp.broadcast_to(jnp.where(batch_id < batches, start, 2 * cells), (SLOTS, 128))
     tail = slot == last[0] - first[0]
-    head = slot == 0.0
+    head = slot == 0
     behind = {h: (last[h] == first[0]).astype(f32) for h in offsets if h < 0}
     ahead = {h: (first[h] == last[0]).astype(f32) for h in offsets if h > 0}
 
+    crowded = jnp.zeros((1, 1), jnp.int32)
+    for inner, room in ((SLOTS - 1, cells), (CLOSE - 1, width)):
+        window = jnp.sum(
+            jnp.where((up >= down) & (up < down + inner), column, 0), axis=0, keepdims=True
+        )
+        window = jnp.where((window < room - 1) & (batch_lane[0:1] <= batches - inner), 1, 0)
+        crowded = crowded + jnp.sum(window, axis=1, keepdims=True)
+    flag_ref[...] = jnp.broadcast_to(crowded, (1, 128))
+
     def inside(c, width, times):
-        position = (
-            lax.broadcasted_iota(jnp.int32, (SLOTS * times, width), 1) + c * width
-        ).astype(f32)
+        position = lax.broadcasted_iota(jnp.int32, (SLOTS * times, width), 1) + c * width
         low = jnp.concatenate([start] * times, axis=0)
         high = jnp.concatenate([stop] * times, axis=0)
         return ((position >= low) & (position < high)).astype(f32)
@@ -428,12 +429,10 @@
             value = jnp.where(row == i, line, value)
         return value
 
-    width = 512
-    per_load = part // width
 
     for i in range(loads):
         columns = pl.ds(i * part, part)
-        pltpu.make_async_copy(z_hbm.at[:, columns], zf.at[:, columns], load_sems.at[i]).wait()
+        pltpu.make_async_copy(z_hbm.at[0, :, columns], zf.at[:, columns], load_sems.at[i]).wait()
 
     def prior_step(c, total):
         columns = pl.ds(pl.multiple_of(c * width, width), width)
@@ -492,39 +491,51 @@
     f3 = factor - f1 - f2
     factor = jnp.concatenate([f1, f2, f3, jnp.zeros_like(f3)], axis=0).T.astype(bf16)
 
-    acc[...] = jnp.zeros_like(acc)
+    def summed(value):
+        top, low = value[0:ROWS], value[ROWS : 2 * ROWS]
+        return top[:, 0:clusters] + top[:, clusters:] + low[:, 0:clusters] + low[:, clusters:]
 
     def moment_step(c, carry):
         columns = pl.ds(pl.multiple_of(c * width, width), width)
-        mask = inside(c, width, 4).astype(bf16)
-        weighed = ex[:, columns] * plain(factor, mask)
+        mask = inside(c, width, 4)
+        weighed = ex[:, columns] * plain(factor, mask.astype(bf16))
         a1, a2 = two_pieces(weighed * (1.0 / jnp.sum(weighed, axis=0, keepdims=True)))
-        pair[0:clusters, columns] = a1
-        pair[clusters : 2 * clusters, columns] = a2
+        both = jnp.concatenate([a1, a2], axis=0)
+        pair[:, columns] = both
         z = zc[:, columns]
-        both = jnp.concatenate([a1, a2], axis=0)
-        lined = jnp.concatenate([z * mask[s : s + 1, :] for s in range(SLOTS)], axis=0)
-        acc[...] += across(lined, both)
+        kind = jnp.sum(mask[0:SLOTS] * slot.astype(f32), axis=0, keepdims=True)
+        kind = kind - base_of(c).astype(f32)
+        lined = [z * (kind == j).astype(f32).astype(bf16) for j in range(CLOSE)]
+        value = across(jnp.concatenate(lined, axis=0), both)
+        for j in range(CLOSE):
+            pieces[c, j] = summed(value[2 * ROWS * j : 2 * ROWS * (j + 1)])
         return carry
 
+    def base_of(c):
+        return jnp.sum(
+            jnp.where((start <= c * width) & (slot > 0) & (batch_id < batches), 1, 0),
+            axis=0,
+            keepdims=True,
+        )
+
     lax.fori_loop(0, cells // width, moment_step, 0)
-    moments = []
-    for s in range(SLOTS):
-        top = acc[2 * ROWS * s : 2 * ROWS * s + ROWS, :]
-        low = acc[2 * ROWS * s + ROWS : 2 * ROWS * (s + 1), :]
-        moments.append(
-            top[:, 0:clusters] + top[:, clusters:] + low[:, 0:clusters] + low[:, clusters:]
-        )
+    moments = [jnp.zeros((ROWS, clusters), f32) for s in range(SLOTS)]
+    for c in range(cells // width):
+        base = base_of(c)
+        for s in range(SLOTS):
+            for j in range(min(s + 1, CLOSE)):
+                moments[s] = moments[s] + jnp.where(base + j == s, 1.0, 0.0) * pieces[c, j]
+    whole = moments[0]
+    for s in range(1, SLOTS):
+        whole = whole + moments[s]
     mass = rows_of(*[moments[s][pcs : pcs + 1] for s in range(SLOTS)])
     near_out[1] = rows_of(
         mass[0:1], jnp.sum(jnp.where(tail, mass, 0.0), axis=0, keepdims=True)
     )
     for i, h in enumerate(offsets):
         push(near_out.at[1], near_mass.at[len(offsets) - 1 - i], 3, neighbour(h))
-    whole = moments[0]
     tail_moment = moments[0] * tail[0:1].astype(f32)
     for s in range(1, SLOTS):
-        whole = whole + moments[s]
         tail_moment = tail_moment + moments[s] * tail[s : s + 1].astype(f32)
     ends_out[0] = moments[0][0:56]
     ends_out[1] = tail_moment[0:56]
@@ -601,19 +612,6 @@
         c1, c2 = two_pieces(jnp.concatenate([slope, jnp.zeros((8, clusters), f32)], axis=0))
         slopes[ROWS * s : ROWS * (s + 1), :] = jnp.concatenate([c1, c1, c2], axis=1)
 
-    def moved_step(c, carry):
-        columns = pl.ds(pl.multiple_of(c * width, width), width)
-        both = pair[:, columns]
-        every = plain(slopes[...], jnp.concatenate([both, both[0:clusters]], axis=0))
-        mask = inside(c, width, 1)
-        moved = every[0:ROWS] * mask[0:1]
-        for s in range(1, SLOTS):
-            moved = moved + every[ROWS * s : ROWS * (s + 1)] * mask[s : s + 1]
-        moved_ref[:, columns] = moved[0:pcs]
-        return carry
-
-    lax.fori_loop(0, cells // width, moved_step, 0)
-
     arrived(full_sums.at[0, pl.ds(1, near - 1)], 9)
     centre = gathered(0)
     centre = (centre / (1.0 + centre[pcs : pcs + 1])).T
@@ -635,6 +633,60 @@
     left(tile_in.at[1], 8)
     left(full_sums.at[0, pl.ds(1, near - 1)], 9)
     left(full_sums.at[1, pl.ds(1, near - 1)], 10)
+
+
+def correct_kernel(
+    zf, pair, slopes, starts_ref, cent_ref, out_hbm, cent_hbm, held, starts, out_sems
+):
+    pcs, cells = zf.shape
+    clusters = pair.shape[0] // 2
+    loads = out_sems.shape[0] - 1
+    part = cells // loads
+    cent = pltpu.make_async_copy(cent_ref, cent_hbm, out_sems.at[loads])
+    cent.start()
+    begin = [jnp.max(starts_ref[s : s + 1, :]) for s in range(SLOTS)]
+    for s in range(SLOTS):
+        starts[s] = begin[s]
+    outs = []
+    lane = lax.broadcasted_iota(jnp.int32, (1, TILE), 1)
+    for i in range(loads):
+        for t in range(i * part // TILE, (i + 1) * part // TILE):
+            columns = slice(t * TILE, (t + 1) * TILE)
+            base = sum((begin[s] <= t * TILE).astype(jnp.int32) for s in range(1, SLOTS))
+            final = sum((begin[s] < (t + 1) * TILE).astype(jnp.int32) for s in range(1, SLOTS))
+            border = jnp.int32(2 * cells)
+            for s in range(1, SLOTS):
+                border = jnp.where(
+                    begin[s] > t * TILE, jnp.minimum(border, begin[s]), border
+                )
+            following = jnp.minimum(base + 1, SLOTS - 1)
+            both = pair[:, columns]
+            both = jnp.concatenate([both, both[0:clusters]], axis=0)
+
+            def slope_of(j):
+                return slopes[pl.ds(pl.multiple_of(j * ROWS, ROWS), ROWS), :]
+
+            moved = plain(jnp.concatenate([slope_of(base), slope_of(following)], axis=0), both)
+            moved = jnp.where(lane < border - t * TILE, moved[0:ROWS], moved[ROWS:])
+            held[:, columns] = zf[:, columns] - moved[0:pcs]
+
+            @pl.when(final > base + 1)
+            def _():
+                def more(j, carry):
+                    other = zf[:, columns] - plain(slope_of(j), both)[0:pcs]
+                    held[:, columns] = jnp.where(
+                        lane >= starts[j] - t * TILE, other, held[:, columns]
+                    )
+                    return carry
+
+                lax.fori_loop(base + 2, final + 1, more, 0)
+
+        columns = pl.ds(i * part, part)
+        outs.append(pltpu.make_async_copy(held.at[:, columns], out_hbm.at[:, columns], out_sems.at[i]))
+        outs[-1].start()
+    for copy in outs:
+        copy.wait()
+    cent.wait()
 
 
 def narrow_body(
@@ -650,13 +702,10 @@
     owned = clusters // (nz * ny * nc)
     vmem = pl.BlockSpec(memory_space=pltpu.VMEM)
     scratch = [
-        pltpu.VMEM((pcs, cells), f32),
         pltpu.VMEM((2 * ROWS, cells), bf16),
         pltpu.VMEM((clusters, cells), f32),
-        pltpu.VMEM((2 * clusters, cells), bf16),
         pltpu.VMEM((clusters, clusters), f32),
-        pltpu.VMEM((SLOTS * 2 * ROWS, 2 * clusters), f32),
-        pltpu.VMEM((SLOTS * ROWS, 3 * clusters), bf16),
+        pltpu.VMEM((cells // 512, CLOSE, ROWS, clusters), f32),
         pltpu.VMEM((2, 8, clusters), f32),
         pltpu.VMEM((2 * reach, 8, clusters), f32),
         pltpu.VMEM((2 * reach, 8, clusters), f32),
@@ -678,45 +727,68 @@
     return pl.pallas_call(
         functools.partial(step_kernel, shape, float(cells * near * far)),
         out_shape=(
-            jax.ShapeDtypeStruct((pcs, cells), f32),
-            jax.ShapeDtypeStruct((owned, pcs), f32),
+            pltpu.VMEM((pcs, cells), f32),
+            pltpu.VMEM((2 * clusters, cells), bf16),
+            pltpu.VMEM((SLOTS * ROWS, 3 * clusters), bf16),
+            pltpu.VMEM((SLOTS, 128), jnp.int32),
+            pltpu.VMEM((1, 128), jnp.int32),
+            pltpu.VMEM((owned, pcs), f32),
         ),
         in_specs=[pl.BlockSpec(memory_space=pl.ANY)] + [vmem] * 4,
-        out_specs=(vmem, vmem),
+        out_specs=(vmem,) * 6,
         scratch_shapes=scratch,
         compiler_params=pltpu.CompilerParams(
-            collective_id=0, has_side_effects=True, vmem_limit_bytes=40 * 1024 * 1024
+            collective_id=0, has_side_effects=True, vmem_limit_bytes=24 * 1024 * 1024
         ),
     )(
-        latent_coordinates,
-        group_means,
+        latent_coordinates[None],
+        group_means.T,
         entropy_scaling.reshape(1, clusters),
         sample_shrinkage_lambda.reshape(1, batches),
         sample_population.reshape(1, batches),
     )
 
 
+def corrected_by(kept, pair, slopes, starts, new_centroids):
+    pcs, cells = kept.shape
+    vmem = pl.BlockSpec(memory_space=pltpu.VMEM)
+    anywhere = pl.BlockSpec(memory_space=pl.ANY)
+    return pl.pallas_call(
+        correct_kernel,
+        out_shape=(pltpu.HBM((pcs, cells), f32), pltpu.HBM(new_centroids.shape, f32)),
+        in_specs=[vmem] * 5,
+        out_specs=(anywhere, anywhere),
+        scratch_shapes=[
+            pltpu.VMEM((pcs, cells), f32),
+            pltpu.SMEM((SLOTS,), jnp.int32),
+            pltpu.SemaphoreType.DMA((5,)),
+        ],
+        compiler_params=pltpu.CompilerParams(vmem_limit_bytes=16 * 1024 * 1024),
+    )(
+        kept,
+        pair,
+        slopes,
+        starts,
+        new_centroids,
+    )
+
+
 def body(
     shape, latent_coordinates, group_means, entropy_scaling, sample_shrinkage_lambda, sample_population
 ):
-    cells = latent_coordinates.shape[1]
-    batches = sample_population.shape[0]
-    inner = SLOTS - 1
-    window = sample_population[: batches - inner + 1]
-    for i in range(1, inner):
-        window = window + sample_population[i : batches - inner + 1 + i]
-    few = jnp.min(window) >= cells - 1
-    moved, new_centroids = lax.cond(
-        few,
-        functools.partial(narrow_body, shape),
-        wide_body,
+    arguments = (
         latent_coordinates,
         group_means,
         entropy_scaling,
         sample_shrinkage_lambda,
         sample_population,
     )
-    return (latent_coordinates - moved, new_centroids)
+    kept, pair, slopes, starts, flag, new_centroids = narrow_body(shape, *arguments)
+    return lax.cond(
+        flag[0, 0] == 0,
+        lambda: corrected_by(kept, pair, slopes, starts, new_centroids),
+        lambda: wide_body(*arguments),
+    )
 
 
 def solution(mesh):

time: 59.3 us -> 55 us (0.927)
  other arithmetic: 3.84 us -> 0 us
  Pallas kernels: 52.2 us -> 53.7 us
  local copies, waits for them, and re-layouts: 1.41 us -> 0 us
    pallas_call x0 -> x1, Pallas kernels: none -> 3.9 us  [corrected_by(): pl.pallas_call(correct_kernel, out_shape=(pltpu.HBM((pcs, cells), f32), p...]
    pallas_call x1, Pallas kernels: 52.2 us -> 49.8 us  [narrow_body(): pl.pallas_call(functools.partial(step_kernel, shape, float(cells * near *...]
    sub x1 -> x0, other arithmetic: 2.2 us -> none  [body(): return (latent_coordinates - moved, new_centroids)]
    reduce_min x1 -> x0, other arithmetic: 1.65 us -> none  [body(): few = jnp.min(window) >= cells - 1]
    another operation x1 -> x0, local copies, waits for them, and re-layouts: 0.85 us -> none
where the time goes in v1:
time: 55 us; the launch traced here: 54.8 us
  Pallas kernels  53.7 us (98%)
  between operations  0.85 us (2%)
    pallas_call x1, Pallas kernels, narrow_body(): pl.pallas_call(functools.partial(step_kernel, shape, float(cells * near *...  49.8 us
    pallas_call x1, Pallas kernels, corrected_by(): pl.pallas_call(correct_kernel, out_shape=(pltpu.HBM((pcs, cells), f32), p...  3.9 us

profile of v1, /device:TPU:1, one launch (start us, length us, event | category | flops | bytes accessed | tf_op | source)
XLA Modules:
  0.0 54.8 jit_solution(14487521269228666323)
XLA Ops:
  0.6 49.8 %shard_map.72 = (f32[50,4096]{1,0:T(8,128)S(1)}, bf16[256,4096]{1,0:T(8,128)(2,1)S(1)}, bf16[512,384]{1,0:T(8,128)(2,1)S(1)}, s32[8,128]{1,0:T(8,128)S(1)}, s32[1,128]{1,0:T(1,128)S(1)}, /*index=5*/f32[2,50]{1,0:T(2,128)S(1)}) custom-call(f32[1,50,4096]{2,1,0:T(8,128)} %bitcast.100, f32[50,128]{1,0:T(8,128)} %bitcast.102, f32[1,128]{1,0:T(1,128)} %bitcast.110, ...), custom_call_target="tpu_custom_call" | custom-call | tf_op jit(solution)/shard_map/pallas_call | solution.py:727
  50.5 4.1 %conditional.1 = ((f32[50,4096]{1,0:T(8,128)}, f32[2,50]{1,0:T(2,128)})) conditional(s32[]{:T(128)} %bitcast.39, (s32[200]{0:T(256)}, f32[128,50]{0,1:T(8,128)}, f32[50,4096]{1,0:T(8,128)}, f32[128]{0:T(128)}, f32[200]{0:T(256)}) %tuple.30, (f32[50,4096]{1,0:T(8,128)S(1)}, bf16[256,4096]{1,0:T(8,128)(2,1)S(1)}, bf16[512,384]{1,0:T(8,128)(2,1)S(1)}, ...), branch_computations={%region_0.42_spmd, %region_42.43_spmd} | conditional | flops 978158016 | bytes 142660992 | solution.py:787
  50.8 3.9 %branch_1_fun.1 = (f32[50,4096]{1,0:T(8,128)}, f32[2,50]{1,0:T(2,128)}) custom-call(f32[50,4096]{1,0:T(8,128)S(1)} %get-tuple-element.147.zf, bf16[256,4096]{1,0:T(8,128)(2,1)S(1)} %get-tuple-element.148.pair, bf16[512,384]{1,0:T(8,128)(2,1)S(1)} %get-tuple-element.149.slopes, s32[8,128]{1,0:T(8,128)S(1)} %get-tuple-element.150.starts_ref, ...), custom_call_target="tpu_custom_call" | custom-call | tf_op jit(solution)/shard_map/cond/branch_1_fun/pallas_call | solution.py:756

commit v2 on v1

--- a/solution.py
+++ b/solution.py
@@ -259,18 +259,23 @@
     shape,
     cells_all,
     z_hbm,
-    means_ref,
-    soft_ref,
-    ridge_ref,
-    pop_ref,
+    means_hbm,
+    soft_hbm,
+    ridge_hbm,
+    pop_hbm,
     zf,
     pair,
     slopes,
     starts_ref,
     flag_ref,
     cent_ref,
+    means_ref,
+    soft_ref,
+    ridge_ref,
+    pop_ref,
     zc,
     ex,
+    lined,
     means_wide,
     pieces,
     near_out,
@@ -278,15 +283,20 @@
     near_mass,
     near_moments,
     ends_out,
+    full_moments,
+    line_out,
     line_a,
     line_b,
     sums_out,
     sum_in,
     cent_out,
     cent_in,
+    cent_y,
+    cent_z,
     tile_out,
     tile_in,
     full_sums,
+    small_sems,
     load_sems,
     send_sems,
     recv_sems,
@@ -315,6 +325,13 @@
     def peer(r):
         return lax.rem(block + r, far) * near + rank
 
+    def along_y(r):
+        at = lax.rem(block, ny)
+        return (block - at + lax.rem(at + r, ny)) * near + rank
+
+    def along_z(r):
+        return lax.rem(block + r * ny, far) * near + rank
+
     def neighbour(h):
         return lax.rem(me + (h + count), count)
 
@@ -334,10 +351,21 @@
     def left(buffer, which):
         pltpu.make_async_copy(buffer, buffer, send_sems.at[which]).wait()
 
-    loads = load_sems.shape[0]
-    part = cells // loads
-    for i in range(loads):
-        columns = pl.ds(i * part, part)
+    small = [
+        pltpu.make_async_copy(src, dst, small_sems.at[i])
+        for i, (src, dst) in enumerate(
+            (
+                (pop_hbm, pop_ref),
+                (means_hbm, means_ref),
+                (soft_hbm, soft_ref),
+                (ridge_hbm, ridge_ref),
+            )
+        )
+    ]
+    for copy in small:
+        copy.start()
+    for i in range(cells // width):
+        columns = pl.ds(i * width, width)
         pltpu.make_async_copy(z_hbm.at[0, :, columns], zf.at[:, columns], load_sems.at[i]).start()
 
     barrier = pltpu.get_barrier_semaphore()
@@ -351,6 +379,13 @@
         return carry
 
     lax.fori_loop(1, far, greet, 0)
+    for r in range(1, ny):
+        pl.semaphore_signal(barrier, inc=1, device_id=along_y(r), device_id_type=LOGICAL)
+    for r in range(1, nz):
+        pl.semaphore_signal(barrier, inc=1, device_id=along_z(r), device_id_type=LOGICAL)
+
+    for copy in small:
+        copy.wait()
 
     means_wide[...] = jnp.zeros_like(means_wide)
     means_wide[0:pcs, :] = means_ref[...]
@@ -412,7 +447,7 @@
         high = jnp.concatenate([stop] * times, axis=0)
         return ((position >= low) & (position < high)).astype(f32)
 
-    def completed(own, buffer, tail_row):
+    def completed(own, buffer):
         before = jnp.zeros((1, clusters), f32)
         after = jnp.zeros((1, clusters), f32)
         for i, h in enumerate(offsets):
@@ -422,20 +457,26 @@
                 after = after + ahead[h] * buffer[i, 0:1, :]
         return own + jnp.where(head, before, 0.0) + jnp.where(tail, after, 0.0)
 
-    def rows_of(*lines):
-        row = lax.broadcasted_iota(jnp.int32, (8, clusters), 0)
-        value = jnp.zeros((8, clusters), f32)
-        for i, line in enumerate(lines):
-            value = jnp.where(row == i, line, value)
-        return value
-
-
-    for i in range(loads):
-        columns = pl.ds(i * part, part)
-        pltpu.make_async_copy(z_hbm.at[0, :, columns], zf.at[:, columns], load_sems.at[i]).wait()
+    def tail_of(value):
+        return jnp.sum(jnp.where(tail, value, 0.0), axis=0, keepdims=True)
+
+    def greeted_rows(which, value):
+        near_out[which, 0:1, :] = value[0:1]
+        near_out[which, 1:2, :] = tail_of(value)
+
+    runs = cells // width
+
+    def base_of(c):
+        return jnp.sum(
+            jnp.where((start <= c * width) & (slot > 0) & (batch_id < batches), 1, 0),
+            axis=0,
+            keepdims=True,
+        )
+
 
     def prior_step(c, total):
         columns = pl.ds(pl.multiple_of(c * width, width), width)
+        pltpu.make_async_copy(z_hbm.at[0, :, columns], zf.at[:, columns], load_sems.at[c]).wait()
         z1, z2 = two_pieces(
             jnp.concatenate(
                 [
@@ -460,29 +501,43 @@
     )
     counts = total[0:SLOTS, 0:clusters] + total[0:SLOTS, clusters : 2 * clusters]
     own_total = jnp.sum(counts, axis=0, keepdims=True)
-    near_out[0] = rows_of(
-        counts[0:1], jnp.sum(jnp.where(tail, counts, 0.0), axis=0, keepdims=True), own_total
-    )
-    pl.semaphore_wait(barrier, near - 1 + far - 1 + len(offsets))
+    greeted_rows(0, counts)
+    line_out[0] = own_total
+    pl.semaphore_wait(barrier, near - 1 + far - 1 + len(offsets) + ny - 1 + nz - 1)
     for r in range(1, near):
-        push(near_out.at[0], line_a.at[r - 1], 0, mate(r))
+        push(line_out.at[0], line_a.at[r - 1], 0, mate(r))
     for i, h in enumerate(offsets):
         push(near_out.at[0], near_counts.at[len(offsets) - 1 - i], 1, neighbour(h))
+
+    def line_step(c, carry):
+        columns = pl.ds(pl.multiple_of(c * width, width), width)
+        mask = inside(c, width, 1)
+        kind = jnp.sum(mask * slot.astype(f32), axis=0, keepdims=True)
+        kind = kind - base_of(c).astype(f32)
+        z = zc[:, columns]
+        for j in range(CLOSE):
+            lined[2 * ROWS * j : 2 * ROWS * (j + 1), columns] = z * (kind == j).astype(
+                f32
+            ).astype(bf16)
+        return carry
+
+    lax.fori_loop(0, runs // 2, line_step, 0)
     arrived(line_a, 0)
     block_total = own_total
     for r in range(near - 1):
-        block_total = block_total + line_a[r, 2:3, :]
-    tile_out[0] = jnp.broadcast_to(block_total, (8, clusters))
+        block_total = block_total + line_a[r]
+    line_out[1] = block_total
 
     def send_line(r, carry):
-        push(tile_out.at[0], line_b.at[r - 1], 2, peer(r))
+        push(line_out.at[1], line_b.at[r - 1], 2, peer(r))
         return carry
 
     lax.fori_loop(1, far, send_line, 0)
+    lax.fori_loop(runs // 2, runs, line_step, 0)
     arrived(near_counts, 1)
-    full_counts = completed(counts, near_counts, 1)
+    full_counts = completed(counts, near_counts)
     arrived(line_b, 2)
-    totals = block_total + jnp.sum(line_b[...], axis=0)[0:1]
+    totals = block_total + jnp.sum(line_b[...], axis=0)
     expected = held * totals * (1.0 / cells_all)
     ratio = (expected + 1.0) / (full_counts + 1.0)
     factor = ratio * ratio
@@ -491,75 +546,75 @@
     f3 = factor - f1 - f2
     factor = jnp.concatenate([f1, f2, f3, jnp.zeros_like(f3)], axis=0).T.astype(bf16)
 
-    def summed(value):
-        top, low = value[0:ROWS], value[ROWS : 2 * ROWS]
-        return top[:, 0:clusters] + top[:, clusters:] + low[:, 0:clusters] + low[:, clusters:]
-
-    def moment_step(c, carry):
+    def assign_step(c, total):
         columns = pl.ds(pl.multiple_of(c * width, width), width)
-        mask = inside(c, width, 4)
-        weighed = ex[:, columns] * plain(factor, mask.astype(bf16))
+        mask = inside(c, width, 4).astype(bf16)
+        weighed = ex[:, columns] * plain(factor, mask)
         a1, a2 = two_pieces(weighed * (1.0 / jnp.sum(weighed, axis=0, keepdims=True)))
         both = jnp.concatenate([a1, a2], axis=0)
         pair[:, columns] = both
-        z = zc[:, columns]
-        kind = jnp.sum(mask[0:SLOTS] * slot.astype(f32), axis=0, keepdims=True)
-        kind = kind - base_of(c).astype(f32)
-        lined = [z * (kind == j).astype(f32).astype(bf16) for j in range(CLOSE)]
-        value = across(jnp.concatenate(lined, axis=0), both)
-        for j in range(CLOSE):
-            pieces[c, j] = summed(value[2 * ROWS * j : 2 * ROWS * (j + 1)])
-        return carry
-
-    def base_of(c):
-        return jnp.sum(
-            jnp.where((start <= c * width) & (slot > 0) & (batch_id < batches), 1, 0),
-            axis=0,
-            keepdims=True,
-        )
-
-    lax.fori_loop(0, cells // width, moment_step, 0)
-    moments = [jnp.zeros((ROWS, clusters), f32) for s in range(SLOTS)]
-    for c in range(cells // width):
-        base = base_of(c)
-        for s in range(SLOTS):
-            for j in range(min(s + 1, CLOSE)):
-                moments[s] = moments[s] + jnp.where(base + j == s, 1.0, 0.0) * pieces[c, j]
-    whole = moments[0]
-    for s in range(1, SLOTS):
-        whole = whole + moments[s]
-    mass = rows_of(*[moments[s][pcs : pcs + 1] for s in range(SLOTS)])
-    near_out[1] = rows_of(
-        mass[0:1], jnp.sum(jnp.where(tail, mass, 0.0), axis=0, keepdims=True)
-    )
+        return total + across(mask[0 : 2 * SLOTS], both)
+
+    total = lax.fori_loop(0, runs, assign_step, jnp.zeros((2 * SLOTS, 2 * clusters), f32))
+    mass = total[0:SLOTS, 0:clusters] + total[0:SLOTS, clusters : 2 * clusters]
+    greeted_rows(1, mass)
     for i, h in enumerate(offsets):
         push(near_out.at[1], near_mass.at[len(offsets) - 1 - i], 3, neighbour(h))
-    tail_moment = moments[0] * tail[0:1].astype(f32)
-    for s in range(1, SLOTS):
-        tail_moment = tail_moment + moments[s] * tail[s : s + 1].astype(f32)
-    ends_out[0] = moments[0][0:56]
-    ends_out[1] = tail_moment[0:56]
+
+    def moment_step(c, carry):
+        columns = pl.ds(pl.multiple_of(c * width, width), width)
+        value = across(lined[:, columns], pair[:, columns])
+        for j in range(CLOSE):
+            top = value[2 * ROWS * j : 2 * ROWS * j + ROWS]
+            low = value[2 * ROWS * j + ROWS : 2 * ROWS * (j + 1)]
+            pieces[c, j] = (
+                top[:, 0:clusters] + top[:, clusters:] + low[:, 0:clusters] + low[:, clusters:]
+            )
+        return carry
+
+    lax.fori_loop(0, runs, moment_step, 0)
+    places = [(c, j) for c in range(runs) for j in range(CLOSE)]
+    whole = pieces[0, 0]
+    for c, j in places[1:]:
+        whole = whole + pieces[c, j]
     for t in range(near):
         cent_out[t] = whole[t * rows_each : (t + 1) * rows_each]
     for r in range(1, near):
         push(cent_out.at[lax.rem(rank + r, near)], cent_in.at[r - 1], 4, mate(r))
     arrived(near_mass, 3)
-    full_mass = completed(mass, near_mass, 1)
+    full_mass = completed(mass, near_mass)
     shrink = ridge / (full_mass + ridge)
-    right = moments[0] * shrink[0:1]
-    for s in range(1, SLOTS):
-        right = right + moments[s] * shrink[s : s + 1]
+    right = jnp.zeros((ROWS, clusters), f32)
+    for c in range(runs):
+        base = base_of(c)
+        for j in range(CLOSE):
+            line = jnp.sum(jnp.where(slot == base + j, shrink, 0.0), axis=0, keepdims=True)
+            right = right + line * pieces[c, j]
     for t in range(near):
         sums_out[t] = right[t * rows_each : (t + 1) * rows_each]
     for r in range(1, near):
         push(sums_out.at[lax.rem(rank + r, near)], sum_in.at[r - 1], 5, mate(r))
+
+    first_moment = pieces[0, 0]
+    for c in range(1, runs):
+        first_moment = first_moment + jnp.where(base_of(c) == 0, 1.0, 0.0) * pieces[c, 0]
+    tail_moment = jnp.zeros((ROWS, clusters), f32)
+    tail_slot = last[0] - first[0]
+    for c in range(runs):
+        base = base_of(c)
+        for j in range(CLOSE):
+            tail_moment = tail_moment + jnp.where(base + j == tail_slot, 1.0, 0.0) * pieces[c, j]
+    ends_out[0] = first_moment[0:56]
+    ends_out[1] = tail_moment[0:56]
     for i, h in enumerate(offsets):
         push(ends_out.at[int(h > 0)], near_moments.at[len(offsets) - 1 - i], 6, neighbour(h))
     arrived(cent_in, 4)
     cent_tile = cent_out[rank]
     for r in range(near - 1):
         cent_tile = cent_tile + cent_in[r]
-    tile_out[1] = cent_tile
+    tile_out[0] = cent_tile
+    for r in range(1, ny):
+        push(tile_out.at[0], cent_y.at[r - 1], 7, along_y(r))
     arrived(sum_in, 5)
     sum_tile = sums_out[rank]
     for r in range(near - 1):
@@ -567,15 +622,23 @@
     tile_out[2] = sum_tile
 
     def send_sum(r, carry):
-        push(tile_out.at[2], tile_in.at[1, r - 1], 8, peer(r))
+        push(tile_out.at[2], tile_in.at[r - 1], 8, peer(r))
         return carry
 
-    def send_cent(r, carry):
-        push(tile_out.at[1], tile_in.at[0, r - 1], 7, peer(r))
-        return carry
-
     lax.fori_loop(1, far, send_sum, 0)
-    lax.fori_loop(1, far, send_cent, 0)
+    arrived(cent_y, 7)
+    for r in range(ny - 1):
+        cent_tile = cent_tile + cent_y[r]
+    tile_out[1] = cent_tile
+    for r in range(1, nz):
+        push(tile_out.at[1], cent_z.at[r - 1], 11, along_z(r))
+    moments = []
+    for s in range(SLOTS):
+        moment = jnp.zeros((ROWS, clusters), f32)
+        for c, j in places:
+            if j <= s <= CLOSE * c + j:
+                moment = moment + jnp.where(base_of(c) + j == s, 1.0, 0.0) * pieces[c, j]
+        moments.append(moment)
 
     arrived(near_moments, 6)
     before = jnp.zeros((56, clusters), f32)
@@ -585,13 +648,18 @@
             before = before + behind[h] * near_moments[i]
         else:
             after = after + ahead[h] * near_moments[i]
-
-    arrived(tile_in.at[1], 8)
-    full_sums[1, 0] = sum_tile + jnp.sum(tile_in[1], axis=0)
+    for s in range(SLOTS):
+        moment = moments[s][0:56] + after * tail[s : s + 1].astype(f32)
+        full_moments[s] = moment + before if s == 0 else moment
+
+    arrived(tile_in, 8)
+    full_sums[1, 0] = sum_tile + jnp.sum(tile_in[...], axis=0)
     for r in range(1, near):
         push(full_sums.at[1, 0], full_sums.at[1, r], 10, mate(r))
-    arrived(tile_in.at[0], 7)
-    full_sums[0, 0] = cent_tile + jnp.sum(tile_in[0], axis=0)
+    arrived(cent_z, 11)
+    for r in range(nz - 1):
+        cent_tile = cent_tile + cent_z[r]
+    full_sums[0, 0] = cent_tile
     for r in range(1, near):
         push(full_sums.at[0, 0], full_sums.at[0, r], 9, mate(r))
 
@@ -604,9 +672,7 @@
     right = gathered(1)
     intercept = (right / (1.0 + right[pcs : pcs + 1]))[0:56]
     for s in range(SLOTS):
-        moment = moments[s][0:56] + after * tail[s : s + 1].astype(f32)
-        if s == 0:
-            moment = moment + before
+        moment = full_moments[s]
         line = full_mass[s : s + 1]
         slope = (moment - line * intercept) / (line + ridge[s : s + 1])
         c1, c2 = two_pieces(jnp.concatenate([slope, jnp.zeros((8, clusters), f32)], axis=0))
@@ -629,8 +695,9 @@
     left(cent_in, 4)
     left(sum_in, 5)
     left(near_moments, 6)
-    left(tile_in.at[0], 7)
-    left(tile_in.at[1], 8)
+    left(cent_y, 7)
+    left(tile_in, 8)
+    left(cent_z, 11)
     left(full_sums.at[0, pl.ds(1, near - 1)], 9)
     left(full_sums.at[1, pl.ds(1, near - 1)], 10)
 
@@ -649,30 +716,42 @@
         starts[s] = begin[s]
     outs = []
     lane = lax.broadcasted_iota(jnp.int32, (1, TILE), 1)
+
+    def slope_of(j):
+        return slopes[pl.ds(pl.multiple_of(j * ROWS, ROWS), ROWS), :]
+
     for i in range(loads):
+        beyond = jnp.int32(0)
         for t in range(i * part // TILE, (i + 1) * part // TILE):
             columns = slice(t * TILE, (t + 1) * TILE)
-            base = sum((begin[s] <= t * TILE).astype(jnp.int32) for s in range(1, SLOTS))
-            final = sum((begin[s] < (t + 1) * TILE).astype(jnp.int32) for s in range(1, SLOTS))
+            base = jnp.int32(0)
+            final = jnp.int32(0)
             border = jnp.int32(2 * cells)
             for s in range(1, SLOTS):
-                border = jnp.where(
-                    begin[s] > t * TILE, jnp.minimum(border, begin[s]), border
-                )
+                base = base + jnp.where(begin[s] <= t * TILE, 1, 0)
+                final = final + jnp.where(begin[s] < (t + 1) * TILE, 1, 0)
+                border = jnp.where(begin[s] > t * TILE, jnp.minimum(border, begin[s]), border)
+            beyond = jnp.maximum(beyond, final - base)
             following = jnp.minimum(base + 1, SLOTS - 1)
             both = pair[:, columns]
             both = jnp.concatenate([both, both[0:clusters]], axis=0)
-
-            def slope_of(j):
-                return slopes[pl.ds(pl.multiple_of(j * ROWS, ROWS), ROWS), :]
-
             moved = plain(jnp.concatenate([slope_of(base), slope_of(following)], axis=0), both)
             moved = jnp.where(lane < border - t * TILE, moved[0:ROWS], moved[ROWS:])
             held[:, columns] = zf[:, columns] - moved[0:pcs]
 
-            @pl.when(final > base + 1)
-            def _():
+        @pl.when(beyond > 1)
+        def _():
+            def tile_of(t, carry):
+                columns = pl.ds(pl.multiple_of(t * TILE, TILE), TILE)
+                base = jnp.int32(0)
+                final = jnp.int32(0)
+                for s in range(1, SLOTS):
+                    base = base + jnp.where(begin[s] <= t * TILE, 1, 0)
+                    final = final + jnp.where(begin[s] < (t + 1) * TILE, 1, 0)
+
                 def more(j, carry):
+                    both = pair[:, columns]
+                    both = jnp.concatenate([both, both[0:clusters]], axis=0)
                     other = zf[:, columns] - plain(slope_of(j), both)[0:pcs]
                     held[:, columns] = jnp.where(
                         lane >= starts[j] - t * TILE, other, held[:, columns]
@@ -680,6 +759,9 @@
                     return carry
 
                 lax.fori_loop(base + 2, final + 1, more, 0)
+                return carry
+
+            lax.fori_loop(i * part // TILE, (i + 1) * part // TILE, tile_of, 0)
 
         columns = pl.ds(i * part, part)
         outs.append(pltpu.make_async_copy(held.at[:, columns], out_hbm.at[:, columns], out_sems.at[i]))
@@ -701,28 +783,39 @@
     reach = (MOST - 2) // cells + 1
     owned = clusters // (nz * ny * nc)
     vmem = pl.BlockSpec(memory_space=pltpu.VMEM)
+    tile = (rows_each, clusters)
     scratch = [
+        pltpu.VMEM((pcs, clusters), f32),
+        pltpu.VMEM((1, clusters), f32),
+        pltpu.VMEM((1, batches), f32),
+        pltpu.VMEM((1, batches), jnp.int32),
         pltpu.VMEM((2 * ROWS, cells), bf16),
         pltpu.VMEM((clusters, cells), f32),
+        pltpu.VMEM((2 * ROWS * CLOSE, cells), bf16),
         pltpu.VMEM((clusters, clusters), f32),
         pltpu.VMEM((cells // 512, CLOSE, ROWS, clusters), f32),
-        pltpu.VMEM((2, 8, clusters), f32),
-        pltpu.VMEM((2 * reach, 8, clusters), f32),
-        pltpu.VMEM((2 * reach, 8, clusters), f32),
+        pltpu.VMEM((2, 2, clusters), f32),
+        pltpu.VMEM((2 * reach, 2, clusters), f32),
+        pltpu.VMEM((2 * reach, 2, clusters), f32),
         pltpu.VMEM((2 * reach, 56, clusters), f32),
         pltpu.VMEM((2, 56, clusters), f32),
-        pltpu.VMEM((near - 1, 8, clusters), f32),
-        pltpu.VMEM((far - 1, 8, clusters), f32),
-        pltpu.VMEM((near, rows_each, clusters), f32),
-        pltpu.VMEM((near - 1, rows_each, clusters), f32),
-        pltpu.VMEM((near, rows_each, clusters), f32),
-        pltpu.VMEM((near - 1, rows_each, clusters), f32),
-        pltpu.VMEM((3, rows_each, clusters), f32),
-        pltpu.VMEM((2, far - 1, rows_each, clusters), f32),
-        pltpu.VMEM((2, near, rows_each, clusters), f32),
+        pltpu.VMEM((SLOTS, 56, clusters), f32),
+        pltpu.VMEM((2, 1, clusters), f32),
+        pltpu.VMEM((near - 1, 1, clusters), f32),
+        pltpu.VMEM((far - 1, 1, clusters), f32),
+        pltpu.VMEM((near, *tile), f32),
+        pltpu.VMEM((near - 1, *tile), f32),
+        pltpu.VMEM((near, *tile), f32),
+        pltpu.VMEM((near - 1, *tile), f32),
+        pltpu.VMEM((ny - 1, *tile), f32),
+        pltpu.VMEM((nz - 1, *tile), f32),
+        pltpu.VMEM((3, *tile), f32),
+        pltpu.VMEM((far - 1, *tile), f32),
+        pltpu.VMEM((2, near, *tile), f32),
         pltpu.SemaphoreType.DMA((4,)),
-        pltpu.SemaphoreType.DMA((11,)),
-        pltpu.SemaphoreType.DMA((11,)),
+        pltpu.SemaphoreType.DMA((cells // 512,)),
+        pltpu.SemaphoreType.DMA((12,)),
+        pltpu.SemaphoreType.DMA((12,)),
     ]
     return pl.pallas_call(
         functools.partial(step_kernel, shape, float(cells * near * far)),
@@ -734,7 +827,7 @@
             pltpu.VMEM((1, 128), jnp.int32),
             pltpu.VMEM((owned, pcs), f32),
         ),
-        in_specs=[pl.BlockSpec(memory_space=pl.ANY)] + [vmem] * 4,
+        in_specs=[pl.BlockSpec(memory_space=pl.ANY)] * 5,
         out_specs=(vmem,) * 6,
         scratch_shapes=scratch,
         compiler_params=pltpu.CompilerParams(

time: 55 us -> 47.1 us (0.86)
  Pallas kernels: 53.7 us -> 45.9 us
    pallas_call x1, Pallas kernels: 49.8 us -> 43.8 us  [narrow_body(): pl.pallas_call(functools.partial(step_kernel, shape, float(cells * near *...]
    pallas_call x1, Pallas kernels: 3.9 us -> 2.15 us  [corrected_by(): pl.pallas_call(correct_kernel, out_shape=(pltpu.HBM((pcs, cells), f32), p...]
where the time goes in v2:
time: 47.1 us; the launch traced here: 47 us
  Pallas kernels  45.9 us (97%)
  between operations  0.85 us (2%)
    pallas_call x1, Pallas kernels, narrow_body(): pl.pallas_call(functools.partial(step_kernel, shape, float(cells * near *...  43.8 us
    pallas_call x1, Pallas kernels, corrected_by(): pl.pallas_call(correct_kernel, out_shape=(pltpu.HBM((pcs, cells), f32), p...  2.15 us

profile of v2, /device:TPU:1, one launch (start us, length us, event | category | flops | bytes accessed | tf_op | source)
XLA Modules:
  0.0 47.0 jit_solution(8281037110602565710)
XLA Ops:
  0.6 43.8 %shard_map.72 = (f32[50,4096]{1,0:T(8,128)S(1)}, bf16[256,4096]{1,0:T(8,128)(2,1)S(1)}, bf16[512,384]{1,0:T(8,128)(2,1)S(1)}, s32[8,128]{1,0:T(8,128)S(1)}, s32[1,128]{1,0:T(1,128)S(1)}, /*index=5*/f32[2,50]{1,0:T(2,128)S(1)}) custom-call(f32[1,50,4096]{2,1,0:T(8,128)} %bitcast.100, f32[50,128]{1,0:T(8,128)} %bitcast.102, f32[1,128]{1,0:T(1,128)} %bitcast.110, ...), custom_call_target="tpu_custom_call" | custom-call | tf_op jit(solution)/shard_map/pallas_call | solution.py:820
  44.4 2.4 %conditional.1 = ((f32[50,4096]{1,0:T(8,128)}, f32[2,50]{1,0:T(2,128)})) conditional(s32[]{:T(128)} %bitcast.39, (s32[200]{0:T(256)}, f32[128,50]{0,1:T(8,128)}, f32[50,4096]{1,0:T(8,128)}, f32[128]{0:T(128)}, f32[200]{0:T(256)}) %tuple.30, (f32[50,4096]{1,0:T(8,128)S(1)}, bf16[256,4096]{1,0:T(8,128)(2,1)S(1)}, bf16[512,384]{1,0:T(8,128)(2,1)S(1)}, ...), branch_computations={%region_0.42_spmd, %region_42.43_spmd} | conditional | flops 978158016 | bytes 142660992 | solution.py:880
  44.7 2.2 %branch_1_fun.1 = (f32[50,4096]{1,0:T(8,128)}, f32[2,50]{1,0:T(2,128)}) custom-call(f32[50,4096]{1,0:T(8,128)S(1)} %get-tuple-element.147.zf, bf16[256,4096]{1,0:T(8,128)(2,1)S(1)} %get-tuple-element.148.pair, bf16[512,384]{1,0:T(8,128)(2,1)S(1)} %get-tuple-element.149.slopes, s32[8,128]{1,0:T(8,128)S(1)} %get-tuple-element.150.starts_ref, ...), custom_call_target="tpu_custom_call" | custom-call | tf_op jit(solution)/shard_map/cond/branch_1_fun/pallas_call | solution.py:849

commit v3 on v2

--- a/solution.py
+++ b/solution.py
@@ -291,6 +291,7 @@
     sum_in,
     cent_out,
     cent_in,
+    shrinks,
     cent_y,
     cent_z,
     tile_out,
@@ -322,6 +323,12 @@
     def mate(r):
         return block * near + lax.rem(rank + r, near)
 
+    plane = near * ny
+    in_plane = lax.rem(me, plane)
+
+    def beside(r):
+        return me - in_plane + lax.rem(in_plane + r, plane)
+
     def peer(r):
         return lax.rem(block + r, far) * near + rank
 
@@ -369,20 +376,10 @@
         pltpu.make_async_copy(z_hbm.at[0, :, columns], zf.at[:, columns], load_sems.at[i]).start()
 
     barrier = pltpu.get_barrier_semaphore()
-    for r in range(1, near):
-        pl.semaphore_signal(barrier, inc=1, device_id=mate(r), device_id_type=LOGICAL)
-    for h in offsets:
-        pl.semaphore_signal(barrier, inc=1, device_id=neighbour(h), device_id_type=LOGICAL)
-
-    def greet(r, carry):
-        pl.semaphore_signal(barrier, inc=1, device_id=peer(r), device_id_type=LOGICAL)
-        return carry
-
-    lax.fori_loop(1, far, greet, 0)
-    for r in range(1, ny):
-        pl.semaphore_signal(barrier, inc=1, device_id=along_y(r), device_id_type=LOGICAL)
-    for r in range(1, nz):
-        pl.semaphore_signal(barrier, inc=1, device_id=along_z(r), device_id_type=LOGICAL)
+    greeted = [along_z(r) for r in range(1, nz)] + [beside(r) for r in range(1, plane)]
+    greeted = greeted + [neighbour(h) for h in offsets]
+    for q in greeted:
+        pl.semaphore_signal(barrier, inc=1, device_id=q, device_id_type=LOGICAL)
 
     for copy in small:
         copy.wait()
@@ -432,6 +429,17 @@
     behind = {h: (last[h] == first[0]).astype(f32) for h in offsets if h < 0}
     ahead = {h: (first[h] == last[0]).astype(f32) for h in offsets if h > 0}
 
+    wide = near - 1 + reach
+    row32 = lax.broadcasted_iota(jnp.int32, (32, 1), 0)
+    device = block * near + lax.rem(row32, 16) - reach
+    limit = device * cells + jnp.where(row32 >= 16, cells - 1, 0)
+    ids = jnp.sum(jnp.where(ends <= limit, 1, 0), axis=1, keepdims=True)
+    ids = jnp.where(device < 0, -9, ids)
+    limit = (block * near + lax.rem(half, 8)) * cells + jnp.where(half >= 8, cells - 1, 0)
+    own_ids = jnp.sum(jnp.where(ends <= limit, 1, 0), axis=1, keepdims=True)
+    own_lane = lax.broadcasted_iota(jnp.int32, (16, batches), 1)
+    own_ridge = jnp.sum(jnp.where(own_lane == own_ids, ridge_ref[...], 0.0), axis=1, keepdims=True)
+
     crowded = jnp.zeros((1, 1), jnp.int32)
     for inner, room in ((SLOTS - 1, cells), (CLOSE - 1, width)):
         window = jnp.sum(
@@ -452,9 +460,9 @@
         after = jnp.zeros((1, clusters), f32)
         for i, h in enumerate(offsets):
             if h < 0:
-                before = before + behind[h] * buffer[i, 1:2, :]
+                before = before + behind[h] * buffer[i][1:2]
             else:
-                after = after + ahead[h] * buffer[i, 0:1, :]
+                after = after + ahead[h] * buffer[i][0:1]
         return own + jnp.where(head, before, 0.0) + jnp.where(tail, after, 0.0)
 
     def tail_of(value):
@@ -503,9 +511,9 @@
     own_total = jnp.sum(counts, axis=0, keepdims=True)
     greeted_rows(0, counts)
     line_out[0] = own_total
-    pl.semaphore_wait(barrier, near - 1 + far - 1 + len(offsets) + ny - 1 + nz - 1)
-    for r in range(1, near):
-        push(line_out.at[0], line_a.at[r - 1], 0, mate(r))
+    pl.semaphore_wait(barrier, len(greeted))
+    for r in range(1, plane):
+        push(line_out.at[0], line_a.at[r - 1], 0, beside(r))
     for i, h in enumerate(offsets):
         push(near_out.at[0], near_counts.at[len(offsets) - 1 - i], 1, neighbour(h))
 
@@ -523,21 +531,15 @@
 
     lax.fori_loop(0, runs // 2, line_step, 0)
     arrived(line_a, 0)
-    block_total = own_total
-    for r in range(near - 1):
-        block_total = block_total + line_a[r]
-    line_out[1] = block_total
-
-    def send_line(r, carry):
-        push(line_out.at[1], line_b.at[r - 1], 2, peer(r))
-        return carry
-
-    lax.fori_loop(1, far, send_line, 0)
+    plane_total = own_total + jnp.sum(line_a[...], axis=0)
+    line_out[1] = plane_total
+    for r in range(1, nz):
+        push(line_out.at[1], line_b.at[r - 1], 2, along_z(r))
     lax.fori_loop(runs // 2, runs, line_step, 0)
     arrived(near_counts, 1)
-    full_counts = completed(counts, near_counts)
+    full_counts = completed(counts, [near_counts[i] for i in range(len(offsets))])
     arrived(line_b, 2)
-    totals = block_total + jnp.sum(line_b[...], axis=0)
+    totals = plane_total + jnp.sum(line_b[...], axis=0)
     expected = held * totals * (1.0 / cells_all)
     ratio = (expected + 1.0) / (full_counts + 1.0)
     factor = ratio * ratio
@@ -558,8 +560,11 @@
     total = lax.fori_loop(0, runs, assign_step, jnp.zeros((2 * SLOTS, 2 * clusters), f32))
     mass = total[0:SLOTS, 0:clusters] + total[0:SLOTS, clusters : 2 * clusters]
     greeted_rows(1, mass)
-    for i, h in enumerate(offsets):
-        push(near_out.at[1], near_mass.at[len(offsets) - 1 - i], 3, neighbour(h))
+    around = 2 * wide + 1
+    for h in range(1, wide + 1):
+        push(near_out.at[1], near_mass.at[(around - 1 - h) % around], 3, neighbour(h))
+        push(near_out.at[1], near_mass.at[(around - 1 + h) % around], 3, neighbour(-h))
+    near_mass[around - 1] = near_out[1]
 
     def moment_step(c, carry):
         columns = pl.ds(pl.multiple_of(c * width, width), width)
@@ -574,38 +579,58 @@
 
     lax.fori_loop(0, runs, moment_step, 0)
     places = [(c, j) for c in range(runs) for j in range(CLOSE)]
-    whole = pieces[0, 0]
-    for c, j in places[1:]:
-        whole = whole + pieces[c, j]
-    for t in range(near):
-        cent_out[t] = whole[t * rows_each : (t + 1) * rows_each]
-    for r in range(1, near):
-        push(cent_out.at[lax.rem(rank + r, near)], cent_in.at[r - 1], 4, mate(r))
-    arrived(near_mass, 3)
-    full_mass = completed(mass, near_mass)
-    shrink = ridge / (full_mass + ridge)
+    tail_slot = last[0] - first[0]
+    alone = jnp.where(tail_slot > 0, 1.0, 0.0)
+    shrink = jnp.where(head | tail, 0.0, ridge / (mass + ridge))
+    first_moment = jnp.zeros((ROWS, clusters), f32)
+    tail_moment = jnp.zeros((ROWS, clusters), f32)
+    whole = jnp.zeros((ROWS, clusters), f32)
     right = jnp.zeros((ROWS, clusters), f32)
     for c in range(runs):
         base = base_of(c)
         for j in range(CLOSE):
+            piece = pieces[c, j]
             line = jnp.sum(jnp.where(slot == base + j, shrink, 0.0), axis=0, keepdims=True)
-            right = right + line * pieces[c, j]
+            right = right + line * piece
+            tail_moment = tail_moment + jnp.where(base + j == tail_slot, 1.0, 0.0) * piece
+            whole = whole + piece
+            if j == 0:
+                first_moment = first_moment + jnp.where(base == 0, 1.0, 0.0) * piece
     for t in range(near):
-        sums_out[t] = right[t * rows_each : (t + 1) * rows_each]
+        inner = slice(t * rows_each, (t + 1) * rows_each)
+        sums_out[t, 0] = right[inner]
+        sums_out[t, 1] = first_moment[inner]
+        sums_out[t, 2] = tail_moment[inner] * alone
+        cent_out[t] = whole[inner]
     for r in range(1, near):
         push(sums_out.at[lax.rem(rank + r, near)], sum_in.at[r - 1], 5, mate(r))
-
-    first_moment = pieces[0, 0]
-    for c in range(1, runs):
-        first_moment = first_moment + jnp.where(base_of(c) == 0, 1.0, 0.0) * pieces[c, 0]
-    tail_moment = jnp.zeros((ROWS, clusters), f32)
-    tail_slot = last[0] - first[0]
-    for c in range(runs):
-        base = base_of(c)
-        for j in range(CLOSE):
-            tail_moment = tail_moment + jnp.where(base + j == tail_slot, 1.0, 0.0) * pieces[c, j]
+    for r in range(1, near):
+        push(cent_out.at[lax.rem(rank + r, near)], cent_in.at[r - 1], 4, mate(r))
     ends_out[0] = first_moment[0:56]
     ends_out[1] = tail_moment[0:56]
+    arrived(near_mass.at[pl.ds(0, around - 1)], 3)
+    full_mass = completed(
+        mass, {i: near_mass[(around - 1 + h) % around] for i, h in enumerate(offsets)}
+    )
+    end_mass = jnp.zeros((16, clusters), f32)
+    for p in range(-reach, near + reach):
+        both = near_mass[lax.rem(p + (2 * around - 1) - rank, around)]
+        one, two = ids[p + reach : p + reach + 1], ids[16 + p + reach : 17 + p + reach]
+        end_mass = end_mass + jnp.where(own_ids == one, both[0:1], 0.0)
+        end_mass = end_mass + jnp.where((own_ids == two) & (two != one), both[1:2], 0.0)
+    end_shrink = own_ridge / (end_mass + own_ridge)
+    for t in range(near):
+        shrinks[t, 0:1, :] = end_shrink[t : t + 1]
+        shrinks[t, 1:2, :] = end_shrink[8 + t : 9 + t]
+    arrived(sum_in, 5)
+    sum_tile = jnp.zeros((rows_each, clusters), f32)
+    for r in range(near):
+        by = shrinks[lax.rem(rank + near - r, near)]
+        got = sums_out[rank] if r == 0 else sum_in[r - 1]
+        sum_tile = sum_tile + got[0] + got[1] * by[0:1] + got[2] * by[1:2]
+    tile_out[2] = sum_tile
+    for r in range(1, far):
+        push(tile_out.at[2], tile_in.at[r - 1], 8, peer(r))
     for i, h in enumerate(offsets):
         push(ends_out.at[int(h > 0)], near_moments.at[len(offsets) - 1 - i], 6, neighbour(h))
     arrived(cent_in, 4)
@@ -615,17 +640,6 @@
     tile_out[0] = cent_tile
     for r in range(1, ny):
         push(tile_out.at[0], cent_y.at[r - 1], 7, along_y(r))
-    arrived(sum_in, 5)
-    sum_tile = sums_out[rank]
-    for r in range(near - 1):
-        sum_tile = sum_tile + sum_in[r]
-    tile_out[2] = sum_tile
-
-    def send_sum(r, carry):
-        push(tile_out.at[2], tile_in.at[r - 1], 8, peer(r))
-        return carry
-
-    lax.fori_loop(1, far, send_sum, 0)
     arrived(cent_y, 7)
     for r in range(ny - 1):
         cent_tile = cent_tile + cent_y[r]
@@ -691,7 +705,7 @@
     left(line_a, 0)
     left(near_counts, 1)
     left(line_b, 2)
-    left(near_mass, 3)
+    left(near_mass.at[pl.ds(0, around - 1)], 3)
     left(cent_in, 4)
     left(sum_in, 5)
     left(near_moments, 6)
@@ -796,17 +810,18 @@
         pltpu.VMEM((cells // 512, CLOSE, ROWS, clusters), f32),
         pltpu.VMEM((2, 2, clusters), f32),
         pltpu.VMEM((2 * reach, 2, clusters), f32),
-        pltpu.VMEM((2 * reach, 2, clusters), f32),
+        pltpu.VMEM((2 * (near - 1 + reach) + 1, 2, clusters), f32),
         pltpu.VMEM((2 * reach, 56, clusters), f32),
         pltpu.VMEM((2, 56, clusters), f32),
         pltpu.VMEM((SLOTS, 56, clusters), f32),
         pltpu.VMEM((2, 1, clusters), f32),
-        pltpu.VMEM((near - 1, 1, clusters), f32),
-        pltpu.VMEM((far - 1, 1, clusters), f32),
+        pltpu.VMEM((near * ny - 1, 1, clusters), f32),
+        pltpu.VMEM((nz - 1, 1, clusters), f32),
+        pltpu.VMEM((near, 3, *tile), f32),
+        pltpu.VMEM((near - 1, 3, *tile), f32),
         pltpu.VMEM((near, *tile), f32),
         pltpu.VMEM((near - 1, *tile), f32),
-        pltpu.VMEM((near, *tile), f32),
-        pltpu.VMEM((near - 1, *tile), f32),
+        pltpu.VMEM((near, 2, clusters), f32),
         pltpu.VMEM((ny - 1, *tile), f32),
         pltpu.VMEM((nz - 1, *tile), f32),
         pltpu.VMEM((3, *tile), f32),

time: 47.1 us -> 47.2 us (level)
  no operation moved by 1% of the time
where the time goes in v3:
time: 47.2 us; the launch traced here: 47.1 us
  Pallas kernels  46 us (97%)
  between operations  0.85 us (2%)
    pallas_call x1, Pallas kernels, narrow_body(): pl.pallas_call(functools.partial(step_kernel, shape, float(cells * near *...  43.9 us
    pallas_call x1, Pallas kernels, corrected_by(): pl.pallas_call(correct_kernel, out_shape=(pltpu.HBM((pcs, cells), f32), p...  2.15 us

profile of v3, /device:TPU:1, one launch (start us, length us, event | category | flops | bytes accessed | tf_op | source)
XLA Modules:
  0.0 47.1 jit_solution(8592643733143997195)
XLA Ops:
  0.6 43.9 %shard_map.72 = (f32[50,4096]{1,0:T(8,128)S(1)}, bf16[256,4096]{1,0:T(8,128)(2,1)S(1)}, bf16[512,384]{1,0:T(8,128)(2,1)S(1)}, s32[8,128]{1,0:T(8,128)S(1)}, s32[1,128]{1,0:T(1,128)S(1)}, /*index=5*/f32[2,50]{1,0:T(2,128)S(1)}) custom-call(f32[1,50,4096]{2,1,0:T(8,128)} %bitcast.100, f32[50,128]{1,0:T(8,128)} %bitcast.102, f32[1,128]{1,0:T(1,128)} %bitcast.110, ...), custom_call_target="tpu_custom_call" | custom-call | tf_op jit(solution)/shard_map/pallas_call | solution.py:835
  44.6 2.4 %conditional.1 = ((f32[50,4096]{1,0:T(8,128)}, f32[2,50]{1,0:T(2,128)})) conditional(s32[]{:T(128)} %bitcast.39, (s32[200]{0:T(256)}, f32[128,50]{0,1:T(8,128)}, f32[50,4096]{1,0:T(8,128)}, f32[128]{0:T(128)}, f32[200]{0:T(256)}) %tuple.30, (f32[50,4096]{1,0:T(8,128)S(1)}, bf16[256,4096]{1,0:T(8,128)(2,1)S(1)}, bf16[512,384]{1,0:T(8,128)(2,1)S(1)}, ...), branch_computations={%region_0.42_spmd, %region_42.43_spmd} | conditional | flops 978158016 | bytes 142660992 | solution.py:895
  44.8 2.2 %branch_1_fun.1 = (f32[50,4096]{1,0:T(8,128)}, f32[2,50]{1,0:T(2,128)}) custom-call(f32[50,4096]{1,0:T(8,128)S(1)} %get-tuple-element.147.zf, bf16[256,4096]{1,0:T(8,128)(2,1)S(1)} %get-tuple-element.148.pair, bf16[512,384]{1,0:T(8,128)(2,1)S(1)} %get-tuple-element.149.slopes, s32[8,128]{1,0:T(8,128)S(1)} %get-tuple-element.150.starts_ref, ...), custom_call_target="tpu_custom_call" | custom-call | tf_op jit(solution)/shard_map/cond/branch_1_fun/pallas_call | solution.py:864
